TPU v7x, 256 devices: a whole 4x4x8 slice. The times are simulated.
256 devices in a mesh: elem: 32 (over z_lo, y, core), band: 8 (over z_hi, x).
Axes of the slice: x: 4, y: 4, z: 8 (z_hi: 2, z_lo: 4; z = z_hi * 4 + z_lo), core: 2. Of those that a mesh axis runs over, the one named last changes fastest.
Arguments:
- y_current: bfloat16 [1024, 64, 2048], P('elem', None, 'band'), may hold values from -6 to 6
- y_previous: bfloat16 [1024, 64, 2048], P('elem', None, 'band'), may hold values from -6 to 6
- h_blocks: bfloat16 [1024, 64, 320], P('elem'), may hold values from -0.3125 to 0.3125
- basis_sizes: int32 [1024], P('elem'), may hold values from 40 to 64
- neighbours: int32 [1024, 4], P('elem'), may hold values from 0 to 1023, as said below
Outputs:
- filtered: bfloat16 [1024, 64, 2048], P('elem', None, 'band')
- margin: float32 [2048, 2048], P('elem', 'band')
Inputs may be any that keep to these rules, and one draw needn't show every extreme that they name: `neighbours`: the elements lie on a periodic grid of 64 x 16; row i lists the elements that share an edge with element i, in the order previous grid row, next grid row, previous column, next column, so adjacency is symmetric. Element g belongs to index g // 32 of elem, whose elements fill 2 consecutive grid rows in some order; a neighbour therefore belongs to the same index or to one of the two beside it, periodically, and exactly 16 of an index's elements have a neighbour on the next index, and 16 on the previous one.
All inputs are finite; a program needn't handle non-finite values.
Results may differ from a plain program's by a relative error of at most 0.018.
Values may be sent and summed in bfloat16 or wider, within the bound.
A program may use at most 64 MiB of HBM per device.

v0:
```python
import jax
import jax.numpy as jnp
from jax import lax
from jax.sharding import Mesh
from jax.sharding import PartitionSpec as P

BMAX = 64
GY = 16
DEGREES = 2
ELEM = ("elem_0", "elem_1", "elem_2")


center_value = 0.3
spectral_half = 1.7


def shifted(block, axis, distance):
    devices = range(lax.axis_size(axis))
    route = [((i - distance) % len(devices), i) for i in devices]
    return lax.ppermute(block, axis, route)


def split_up(array, dim, size):
    before, after = (array.shape[:dim], array.shape[dim + 1 :])
    return jnp.moveaxis(array.reshape(*before, size, -1, *after), dim, 0)


def sum_by_chip(array, chips, core, dim):
    sizes = (lax.axis_size(chips), lax.axis_size(core))
    pieces = split_up(array, dim, sizes[0] * sizes[1])
    inside = pieces.shape[1:]
    pieces = pieces.reshape(*sizes, *inside).swapaxes(0, 1).reshape(-1, *inside)
    pieces = lax.psum_scatter(pieces, core, scatter_dimension=0, tiled=True)
    return lax.psum_scatter(pieces, chips, scatter_dimension=0, tiled=True)[0]


def sent_and_summed(array, axis, dim):
    pieces = split_up(array, dim, lax.axis_size(axis))
    arrived = lax.all_to_all(pieces, axis, split_axis=0, concat_axis=0, tiled=True)
    return arrived.astype(jnp.float32).sum(axis=0)


def referenced_slots(relative, local_index, wanted, local_count):
    positions = jnp.arange(local_count, dtype=jnp.int32)
    marked = jnp.where(relative == wanted, local_index, -1)
    present = jnp.any(marked[:, :, None] == positions[None, None, :], axis=(0, 1))
    return jnp.cumsum(present.astype(jnp.int32)) - 1


def on_device(y_current, y_previous, h_blocks, basis_sizes, neighbours):
    local_count = neighbours.shape[0]
    band_width = y_current.shape[2]
    count_elem = lax.axis_size(ELEM)
    myself = lax.axis_index(ELEM)
    owners = neighbours // local_count
    local_index = neighbours % local_count
    relative = (owners - myself + 1) % count_elem - 1
    send_next = jnp.nonzero(jnp.any(relative == 1, axis=1), size=GY)[0]
    send_prev = jnp.nonzero(jnp.any(relative == -1, axis=1), size=GY)[0]
    slot_prev = referenced_slots(relative, local_index, -1, local_count)
    slot_next = referenced_slots(relative, local_index, 1, local_count)
    pool_index = jnp.where(
        relative == 0,
        local_index,
        jnp.where(
            relative == -1,
            local_count + jnp.take(slot_prev, local_index),
            local_count + GY + jnp.take(slot_next, local_index),
        ),
    )
    row_mask = (jnp.arange(BMAX, dtype=jnp.int32)[None, :] < basis_sizes[:, None]).astype(
        jnp.bfloat16
    )[:, :, None]
    mask_float = row_mask.astype(jnp.float32)
    current = y_current * row_mask
    previous = y_previous * row_mask
    for degree in range(DEGREES):
        from_prev = shifted(current[send_next], ELEM, 1)
        from_next = shifted(current[send_prev], ELEM, -1)
        pool = jnp.concatenate([current, from_prev, from_next], axis=0)
        nearby = pool[pool_index]
        stacked = jnp.concatenate([current[:, None], nearby], axis=1).reshape(
            local_count, 5 * BMAX, band_width
        )
        applied = jnp.einsum("irc,icb->irb", h_blocks, stacked, preferred_element_type=jnp.float32)
        following = mask_float * (
            2.0 / spectral_half * (applied - center_value * current.astype(jnp.float32))
            - previous.astype(jnp.float32)
        )
        previous = current
        current = following.astype(jnp.bfloat16)
    flat = current.reshape(local_count * BMAX, band_width)
    spread = lax.all_to_all(flat, "band", split_axis=0, concat_axis=1, tiled=True)
    partial_value = sum_by_chip(
        lax.dot_general(
            spread, spread, (((0,), (0,)), ((), ())), preferred_element_type=jnp.float32
        ).astype(jnp.bfloat16),
        ("elem_0", "elem_1"),
        "elem_2",
        0,
    ).astype(jnp.float32)
    summed = sent_and_summed(partial_value.astype(jnp.bfloat16), "band", 1)
    margin = summed / jnp.float32(local_count * count_elem * BMAX)
    return (current, margin)


def solution(mesh):
    split = Mesh(
        mesh.devices.reshape(4, 4, 2, mesh.shape["band"]), ("elem_0", "elem_1", "elem_2", "band")
    )
    return jax.shard_map(
        on_device,
        mesh=split,
        in_specs=(
            P(ELEM, None, "band"),
            P(ELEM, None, "band"),
            P(ELEM, None, None),
            P(ELEM),
            P(ELEM, None),
        ),
        out_specs=(P(ELEM, None, "band"), P(ELEM, "band")),
        check_vma=False,
    )
```

profile of v0, /device:TPU:2, one launch (start us, length us, event | category | flops | bytes accessed | tf_op | source)
XLA Modules:
  0.0 264.8 jit_solution(4941959711871835336)
XLA Ops:
  7.2 0.9 copy.48
  8.2 0.1 reduce_or.36
  8.3 0.6 convert_reduce_fusion.2
  8.9 0.7 fusion.27
  9.8 0.1 fusion.14
  9.9 0.8 scatter_custom_fusion
  10.8 0.8 fusion.25
  11.6 1.6 broadcast_multiply_fusion
  13.1 0.6 gather_fusion
  13.8 0.1 fusion.32
  13.9 0.6 convert_reduce_fusion.1
  14.7 0.1 fusion.15
  14.8 0.8 scatter_custom_fusion.1
  15.7 0.8 fusion.26
  16.5 1.4 gather_fusion.1
  17.9 6.5 %collective-permute-start.1 = (bf16[16,64,256]{2,1,0:T(8,128)(2,1)}, bf16[16,64,256]{2,1,0:T(8,128)(2,1)}, u32[]{:S(2)}, u32[]{:S(2)}) collective-permute-start(bf16[16,64,256]{2,1,0:T(8,128)(2,1)} %gather_fusion.1), channel_id=1, source_target_pairs={{8,0},{16,8},{24,16},{32,24},{40,32},{48,40},{56,48},{64,56},{72,6... | collective-permute-start | bytes 1572872 | tf_op jit(solution)/shard_map/ppermute | solution.py:20
  24.5 0.1 fusion.8
  24.8 0.1 add_reduce_fusion.1
  25.0 0.1 fusion.9
  25.1 0.1 reshape.416
  25.2 1.2 gather_fusion.6
  26.7 0.1 add_reduce_fusion
  26.8 1.2 gather_fusion.7
  28.0 0.1 reshape.423
  28.2 0.1 reshape.362
  28.3 2.5 fusion.40
  30.8 0.6 collective-permute-done.1
  31.4 2.8 %pad_maximum_fusion.2 = bf16[64,64,256]{2,1,0:T(8,128)(2,1)} fusion(bf16[16,64,256]{2,1,0:T(8,128)(2,1)} %collective-permute-done.1, bf16[16,64,256]{2,1,0:T(8,128)(2,1)} %collective-permute-done, bf16[32,64,256]{2,1,0:T(8,128)(2,1)S(1)} %broadcast_multiply_fusion), kind=kLoop, calls=%fused_computation.22 | loop fusion | flops 2097152 | bytes 4194304 | tf_op jit(solution)/shard_map/concatenate | solution.py:80
  34.2 4.3 %gather_fusion.2 = bf16[128,64,256]{2,1,0:T(8,128)(2,1)} fusion(bf16[64,64,256]{2,1,0:T(8,128)(2,1)} %pad_maximum_fusion.2, s32[1024]{0:T(1024)S(1)} %pad_clamp_fusion), kind=kCustom, calls=%fused_computation.4 | custom fusion | bytes 8389120 | tf_op jit(solution)/shard_map/gather | solution.py:81
  38.5 3.0 %pad_maximum_fusion = bf16[32,5,64,256]{3,2,1,0:T(8,128)(2,1)S(1)} fusion(bf16[32,4,64,256]{3,2,1,0:T(8,128)(2,1)} %bitcast.54, bf16[32,1,64,256]{3,2,1,0:T(8,128)(2,1)} %fusion.40), kind=kLoop, calls=%fused_computation.11 | loop fusion | flops 2621440 | bytes 10485760 | tf_op jit(solution)/shard_map/concatenate | solution.py:82
  41.6 2.3 fusion.4
  43.9 1.8 gather_fusion.4
  45.8 2.6 gather_fusion.3
  48.4 5.8 %collective-permute-start.3 = (bf16[16,64,256]{2,1,0:T(8,128)(2,1)S(1)}, bf16[16,64,256]{2,1,0:T(8,128)(2,1)S(1)}, u32[]{:S(2)}, u32[]{:S(2)}) collective-permute-start(bf16[16,64,256]{2,1,0:T(8,128)(2,1)S(1)} %gather_fusion.4), channel_id=1, source_target_pairs={{8,0},{16,8},{24,16},{32,24},{40,32},{48,40},{56,48},{64,56},{72,6... | collective-permute-start | bytes 1572872 | tf_op jit(solution)/shard_map/ppermute | solution.py:20
  54.2 7.1 %collective-permute-done.2 = bf16[16,64,256]{2,1,0:T(8,128)(2,1)S(1)} collective-permute-done((bf16[16,64,256]{2,1,0:T(8,128)(2,1)}, bf16[16,64,256]{2,1,0:T(8,128)(2,1)S(1)}, u32[]{:S(2)}, u32[]{:S(2)}) %collective-permute-start.2) | collective-permute-done | bytes 524320 | tf_op jit(solution)/shard_map/ppermute | solution.py:20
  61.2 2.8 %pad_maximum_fusion.3 = bf16[64,64,256]{2,1,0:T(8,128)(2,1)} fusion(bf16[16,64,256]{2,1,0:T(8,128)(2,1)S(1)} %collective-permute-done.3, bf16[16,64,256]{2,1,0:T(8,128)(2,1)S(1)} %collective-permute-done.2, bf16[32,64,256]{2,1,0:T(8,128)(2,1)} %fusion.4), kind=kLoop, calls=%fused_computation.23 | loop fusion | flops 2097152 | bytes 4194304 | tf_op jit(solution)/shard_map/concatenate | solution.py:80
  64.0 4.3 %gather_fusion.5 = bf16[128,64,256]{2,1,0:T(8,128)(2,1)} fusion(bf16[64,64,256]{2,1,0:T(8,128)(2,1)} %pad_maximum_fusion.3, s32[1024]{0:T(1024)S(1)} %pad_clamp_fusion), kind=kCustom, calls=%fused_computation.7 | custom fusion | bytes 8389120 | tf_op jit(solution)/shard_map/gather | solution.py:81
  68.4 3.0 %pad_maximum_fusion.1 = bf16[32,5,64,256]{3,2,1,0:T(8,128)(2,1)S(1)} fusion(bf16[32,4,64,256]{3,2,1,0:T(8,128)(2,1)} %bitcast.55, bf16[32,1,64,256]{3,2,1,0:T(8,128)(2,1)} %bitcast.51), kind=kLoop, calls=%fused_computation.12 | loop fusion | flops 2621440 | bytes 10485760 | tf_op jit(solution)/shard_map/concatenate | solution.py:82
  71.4 2.3 fusion.6
  73.7 1.5 copy.62
  75.2 31.7 %all_to_all.24 = bf16[8,256,256]{1,2,0:T(8,128)(2,1)S(1)} all-to-all(bf16[8,256,256]{1,2,0:T(8,128)(2,1)S(1)} %copy.62), channel_id=1, replica_groups=mesh['elem_0'=4,'elem_1'=4,'elem_2'=2,'band'=8] {'band'}, dimensions={0} | all-to-all | bytes 2097152 | tf_op jit(solution)/shard_map/all_to_all | solution.py:93
  106.9 5.6 %convolution_convert_fusion = bf16[2048,2048]{1,0:T(8,128)(2,1)} fusion(bf16[256,2048]{0,1:T(8,128)(2,1)S(1)} %bitcast.56), kind=kOutput, calls=%fused_computation.10 | convolution fusion | flops 2151677952 | bytes 9437184 | tf_op jit(solution)/shard_map/dot_general | solution.py:95
  112.5 8.3 %copy.63 = bf16[16,2,64,2048]{3,2,0,1:T(8,128)(2,1)} copy(bf16[16,2,64,2048]{3,2,1,0:T(8,128)(2,1)} %bitcast.49) | data formatting | bytes 16777216 | tf_op jit(solution)/shard_map/reshape;reshape | solution.py:32
  120.8 20.2 %reduce-scatter.3.cloned.1.call-done = bf16[16,64,2048]{2,1,0:T(8,128)(2,1)} async-done(((bf16[32,64,2048]{2,1,0:T(8,128)(2,1)}), bf16[16,64,2048]{2,1,0:T(8,128)(2,1)}) %reduce-scatter.3.cloned.1.call-update) | async-done | bytes 4194320 | tf_op jit(solution)/shard_map/reduce_scatter | solution.py:33
  141.0 100.6 %reduce-scatter.5.cloned.1.call-done = bf16[1,64,2048]{2,1,0:T(8,128)(2,1)} async-done(((bf16[16,64,2048]{2,1,0:T(8,128)(2,1)}), bf16[1,64,2048]{2,1,0:T(8,128)(2,1)}) %reduce-scatter.5.cloned.1.call-update) | async-done | bytes 262160 | tf_op jit(solution)/shard_map/reduce_scatter | solution.py:34
  241.6 1.0 copy.65
  242.6 14.7 %all_to_all.25 = bf16[8,64,256]{2,1,0:T(8,128)(2,1)S(1)} all-to-all(bf16[8,64,256]{2,1,0:T(8,128)(2,1)S(1)} %bitcast.59), channel_id=1, replica_groups=mesh['elem_0'=4,'elem_1'=4,'elem_2'=2,'band'=8] {'band'}, dimensions={0} | all-to-all | bytes 524288 | tf_op jit(solution)/shard_map/all_to_all | solution.py:39
  257.4 0.6 broadcast_multiply_fusion.1
  (43 shorter events, 1.5 us)
Async XLA Ops:
  7.2 34.4 %copy-start = (bf16[32,64,320]{2,1,0:T(8,128)(2,1)S(1)}, bf16[32,64,320]{2,1,0:T(8,128)(2,1)}, u32[]{:S(2)}) copy-start(bf16[32,64,320]{2,1,0:T(8,128)(2,1)} %param.9) | copy-start | bytes 3932164
  7.2 133.8 %reduce-scatter.3.cloned.1.call-start = ((), (), s32[]{:S(2)}) async-start(), calls=%async_computation.4 | async-start | bytes 12582912 | tf_op jit(solution)/shard_map/reduce_scatter | solution.py:33
  13.7 17.1 %collective-permute-start = (bf16[16,64,256]{2,1,0:T(8,128)(2,1)S(1)}, bf16[16,64,256]{2,1,0:T(8,128)(2,1)}, u32[]{:S(2)}, u32[]{:S(2)}) collective-permute-start(bf16[16,64,256]{2,1,0:T(8,128)(2,1)S(1)} %gather_fusion), channel_id=1, source_target_pairs={{248,0},{0,8},{8,16},{16,24},{24,32},{32,40},{40,48},{48,56},{56,6... | collective-permute-start | bytes 1572872 | tf_op jit(solution)/shard_map/ppermute | solution.py:20
  17.9 13.5 %collective-permute-start.1 = (bf16[16,64,256]{2,1,0:T(8,128)(2,1)}, bf16[16,64,256]{2,1,0:T(8,128)(2,1)}, u32[]{:S(2)}, u32[]{:S(2)}) collective-permute-start(bf16[16,64,256]{2,1,0:T(8,128)(2,1)} %gather_fusion.1), channel_id=1, source_target_pairs={{8,0},{16,8},{24,16},{32,24},{40,32},{48,40},{56,48},{64,56},{72,6... | collective-permute-start | bytes 1572872 | tf_op jit(solution)/shard_map/ppermute | solution.py:20
  38.5 3.0 %copy-start.2 = (bf16[32,64,256]{2,1,0:T(8,128)(2,1)S(1)}, bf16[32,64,256]{2,1,0:T(8,128)(2,1)}, u32[]{:S(2)}) copy-start(bf16[32,64,256]{2,1,0:T(8,128)(2,1)} %param.8) | copy-start | bytes 3145732
  48.3 12.9 %collective-permute-start.2 = (bf16[16,64,256]{2,1,0:T(8,128)(2,1)}, bf16[16,64,256]{2,1,0:T(8,128)(2,1)S(1)}, u32[]{:S(2)}, u32[]{:S(2)}) collective-permute-start(bf16[16,64,256]{2,1,0:T(8,128)(2,1)} %gather_fusion.3), channel_id=1, source_target_pairs={{248,0},{0,8},{8,16},{16,24},{24,32},{32,40},{40,48},{48,56},{56,6... | collective-permute-start | bytes 1572872 | tf_op jit(solution)/shard_map/ppermute | solution.py:20
  48.4 12.9 %collective-permute-start.3 = (bf16[16,64,256]{2,1,0:T(8,128)(2,1)S(1)}, bf16[16,64,256]{2,1,0:T(8,128)(2,1)S(1)}, u32[]{:S(2)}, u32[]{:S(2)}) collective-permute-start(bf16[16,64,256]{2,1,0:T(8,128)(2,1)S(1)} %gather_fusion.4), channel_id=1, source_target_pairs={{8,0},{16,8},{24,16},{32,24},{40,32},{48,40},{56,48},{64,56},{72,6... | collective-permute-start | bytes 1572872 | tf_op jit(solution)/shard_map/ppermute | solution.py:20
  68.4 3.0 %copy-start.1 = (bf16[32,64,256]{2,1,0:T(8,128)(2,1)S(1)}, bf16[32,64,256]{2,1,0:T(8,128)(2,1)}, u32[]{:S(2)}) copy-start(bf16[32,64,256]{2,1,0:T(8,128)(2,1)} %fusion.4) | copy-start | bytes 3145732
  120.8 120.8 %reduce-scatter.5.cloned.1.call-start = ((), (), s32[]{:S(2)}) async-start(), calls=%async_computation.5 | async-start | bytes 4456448 | tf_op jit(solution)/shard_map/reduce_scatter | solution.py:34
Sparse Core Ops, SparseCore 0:
  120.9 20.0 reduce-scatter.2
  143.5 97.9 reduce-scatter.4
where the time goes:
time: 265 us
  waiting for transfers between devices  128 us (48%)
  blocking collectives  46.4 us (18%)
  local copies, waits for them, and re-layouts  30.2 us (11%)
  other arithmetic  22.8 us (9%)
  between operations  14.2 us (5%)
  starting transfers between devices  12.5 us (5%)
  matrix products  10.2 us (4%)
    reduce_scatter x1, waiting for transfers between devices, sum_by_chip(): return lax.psum_scatter(pieces, chips, scatter_dimension=0, tiled=True)[0]  101 us
    all_to_all x1, blocking collectives, on_device(): lax.all_to_all(flat, 'band', split_axis=0, concat_axis=1, tiled=True)  31.7 us
    reduce_scatter x1, waiting for transfers between devices, sum_by_chip(): pieces = lax.psum_scatter(pieces, core, scatter_dimension=0, tiled=True)  20.2 us
    all_to_all x1, blocking collectives, sent_and_summed(): lax.all_to_all(pieces, axis, split_axis=0, concat_axis=0, tiled=True)  14.7 us
    ppermute x4, starting transfers between devices, shifted(): return lax.ppermute(block, axis, route)  12.4 us
    gather x2, local copies, waits for them, and re-layouts, on_device(): nearby = pool[pool_index]  8.66 us
    another operation x1, local copies, waits for them, and re-layouts, sum_by_chip(): pieces = pieces.reshape(*sizes, *inside).swapaxes(0, 1).reshape(-1, *inside)  8.26 us
    ppermute x4, waiting for transfers between devices, shifted(): return lax.ppermute(block, axis, route)  7.69 us
  transfers between devices with their start and end apart: 6, of which 4 were waited for; matrix products, arithmetic and copies ran while one was open for 4% of the time, Pallas kernels for 0%

commit v1 on v0

v1 whole, which is shorter than its diff:
```python
import jax
import jax.numpy as jnp
from jax import lax
from jax.experimental import pallas as pl
from jax.experimental.pallas import tpu as pltpu
from jax.sharding import Mesh
from jax.sharding import PartitionSpec as P

BMAX = 64
EL = 32
GY = 16
BD = 256
NB = 2048
ROWS = GY * BMAX
CH = 4
NCH = GY // CH

CENTER = 0.3
SCALE = 2.0 / 1.7

ELEM = ("zl", "y", "c")
BAND = ("zh", "x")
BF = jnp.bfloat16
F32 = jnp.float32
MESH_ID = pl.DeviceIdType.MESH


def tables_kernel(nb, sizes, tbl, slot, mark, rank):
    me = (lax.axis_index("zl") * 4 + lax.axis_index("y")) * 2 + lax.axis_index("c")

    def clear(i, _):
        mark[i] = 0
        return 0

    lax.fori_loop(0, 2 * EL, clear, 0)

    def place(i, ones):
        row = jnp.where(nb[i, 0] >> 5 == me, 1, 0)
        at = jnp.where(row == 1, GY + ones, i - ones)
        slot[i] = at
        tbl[at, 0] = i
        tbl[at, 1] = sizes[i]
        tbl[i, 6] = at
        mark[row * EL + (nb[i, row] & (EL - 1))] = 1
        return ones + row

    lax.fori_loop(0, EL, place, 0)

    def count(i, seen):
        rank[i] = seen
        return seen + mark[i]

    lax.fori_loop(0, 2 * EL, count, 0)

    def fill(i, _):
        at = slot[i]
        row = at >> 4
        tbl[at, 2] = slot[nb[i, 1 - row] & (EL - 1)]
        tbl[at, 3] = slot[nb[i, 2] & (EL - 1)]
        tbl[at, 4] = slot[nb[i, 3] & (EL - 1)]
        tbl[at, 5] = rank[row * EL + (nb[i, row] & (EL - 1))] - row * GY
        return 0

    lax.fori_loop(0, EL, fill, 0)


def make_tables(neighbours, basis_sizes):
    smem = pl.BlockSpec(memory_space=pltpu.SMEM)
    return pl.pallas_call(
        tables_kernel,
        out_shape=jax.ShapeDtypeStruct((EL, 8), jnp.int32),
        in_specs=[smem, smem],
        out_specs=smem,
        scratch_shapes=[
            pltpu.SMEM((EL,), jnp.int32),
            pltpu.SMEM((2 * EL,), jnp.int32),
            pltpu.SMEM((2 * EL,), jnp.int32),
        ],
    )(neighbours, basis_sizes)


def main_kernel(
    tbl, yc_h, yp_h, h_h, out_f, out_m,
    yc, yp, hv, cur0, cur1, far_p0, far_n0, far_p1, far_n1, acc, fil, outv, xg, pb, rc, s1, ry, s2, rz, mv,
    lsem, hsend, hrecv, zsend, zrecv, xsend, xrecv, csend, crecv, ysend, yrecv, rsend, rrecv,
):
    zl, y, c = (lax.axis_index(a) for a in ELEM)
    zh, x = (lax.axis_index(a) for a in BAND)
    z = zh * 4 + zl
    e = (zl * 4 + y) * 2 + c

    def elem_id(other):
        return {"zl": other // 8, "y": (other // 2) % 4, "c": other % 2}

    def z_id(other):
        return {"zh": other // 4, "zl": other % 4}

    nxt, prv = elem_id((e + 1) % 32), elem_id((e + 31) % 32)
    xp, xm = {"x": (x + 1) % 4}, {"x": (x + 3) % 4}

    def remote(src, dst, ss, rs, to):
        return pltpu.make_async_remote_copy(
            src_ref=src, dst_ref=dst, send_sem=ss, recv_sem=rs, device_id=to, device_id_type=MESH_ID
        )

    load_c = pltpu.make_async_copy(yc_h, yc, lsem.at[0])
    load_p = pltpu.make_async_copy(yp_h, yp, lsem.at[1])
    load_h = pltpu.make_async_copy(h_h, hv, lsem.at[2])
    load_c.start()
    load_h.start()
    load_p.start()

    barrier = pltpu.get_barrier_semaphore()
    partners = [nxt, prv, xp, xm]
    partners += [{"y": (y + d) % 4} for d in (1, 2, 3)]
    partners += [z_id((z + d) % 8) for d in range(1, 8)]
    for to in partners:
        pl.semaphore_signal(barrier, inc=1, device_id=to, device_id_type=MESH_ID)

    rows = lax.broadcasted_iota(jnp.int32, (BMAX, BD), 0)
    zero = jnp.zeros((BMAX, BD), BF)

    load_c.wait()

    def pack(p, _):
        value = yc[tbl[p, 0]].astype(F32)
        cur0[p] = jnp.where(rows < tbl[p, 1], value, 0.0).astype(BF)
        return 0

    lax.fori_loop(GY, EL, pack, 0)
    pl.semaphore_wait(barrier, len(partners))

    halo = ((far_p0, far_n0), (far_p1, far_n1))

    def halo_copies(cur, degree):
        up = remote(cur.at[pl.ds(GY, GY)], halo[degree][0], hsend.at[degree, 0], hrecv.at[degree, 0], nxt)
        down = remote(cur.at[pl.ds(0, GY)], halo[degree][1], hsend.at[degree, 1], hrecv.at[degree, 1], prv)
        return up, down

    up0, down0 = halo_copies(cur0, 0)
    up0.start()
    lax.fori_loop(0, GY, pack, 0)
    down0.start()
    load_h.wait()
    load_p.wait()

    def local_part(cur, prev_of, row):
        def one(p, _):
            i = tbl[p, 0]
            own, n2, n3, n4 = cur[p], cur[tbl[p, 2]], cur[tbl[p, 3]], cur[tbl[p, 4]]
            pair = [zero, n2] if row == 0 else [n2, zero]
            stack = jnp.concatenate([own] + pair + [n3, n4], axis=0)
            applied = jnp.dot(hv[i], stack, preferred_element_type=F32)
            acc[p] = SCALE * (applied - CENTER * own.astype(F32)) - prev_of(p, i).astype(F32)
            return 0

        lax.fori_loop(row * GY, row * GY + GY, one, 0)

    def full_value(p, row, degree):
        i = tbl[p, 0]
        far = halo[degree][row][tbl[p, 5]]
        if row == 0:
            applied = jnp.dot(hv[i, :, 0:128], jnp.concatenate([zero, far], axis=0), preferred_element_type=F32)
        else:
            applied = jnp.dot(hv[i, :, 128:256], jnp.concatenate([far, zero], axis=0), preferred_element_type=F32)
        return jnp.where(rows < tbl[p, 1], acc[p] + SCALE * applied, 0.0).astype(BF)

    for row in (1, 0):
        local_part(cur0, lambda p, i: yp[i], row)

    up1, down1 = halo_copies(cur1, 1)

    def first(row):
        def one(p, _):
            cur1[p] = full_value(p, row, 0)
            return 0

        lax.fori_loop(row * GY, row * GY + GY, one, 0)

    down0.wait_recv()
    first(1)
    up1.start()
    up0.wait_recv()
    first(0)
    down1.start()

    for row in (1, 0):
        local_part(cur1, lambda p, i: cur0[p], row)
    down1.wait_recv()
    up1.wait_recv()

    def z_copy(half, j, src_zh):
        part = pl.ds(j * CH, CH)
        return remote(
            fil.at[pl.ds(half * GY + j * CH, CH)], xg.at[0, src_zh, part], zsend.at[half, j], zrecv.at[src_zh, j],
            z_id((zl + 2 + 4 * half) % 8),
        )

    def second(j, _):
        for row in (1, 0):
            for k in range(CH):
                p = row * GY + j * CH + k
                fil[p] = full_value(p, row, 1)
            z_copy(row, j, zh).start()
        return 0

    lax.fori_loop(0, NCH, second, 0)

    def put(i, _):
        s = tbl[i, 6]
        outv[i] = fil[s]
        return 0

    lax.fori_loop(0, EL, put, 0)
    store_f = pltpu.make_async_copy(outv, out_f, lsem.at[3])
    store_f.start()

    def x_copy(stage, j, h):
        part = pl.ds(j * CH, CH)
        src = 0 if stage < 2 else stage - 1
        dst = (1, 2, 3, 3)[stage]
        to = (xp, xm, xp, xm)[stage]
        sem = stage if stage < 2 else 2
        return remote(xg.at[src, h, part], xg.at[dst, h, part], xsend.at[sem, j, h], xrecv.at[sem, j, h], to)

    def forward(j):
        for h in (0, 1):
            x_copy(0, j, h).wait_recv()
            x_copy(1, j, h).wait_recv()
            x_copy(2 if j < NCH // 2 else 3, j, h).start()

    for j in range(NCH):
        for h in (0, 1):
            z_copy(0, j, h).wait_recv()
            x_copy(0, j, h).start()
            x_copy(1, j, h).start()
        if j > 0:
            forward(j - 1)
    forward(NCH - 1)

    def c_copy(b_a):
        at_zl, at_y = b_a // 2, pl.ds((b_a % 2) * 2, 2)
        return remote(
            pb.at[1 - c, at_zl, at_y], rc.at[at_zl, at_y], csend.at[b_a], crecv.at[b_a], {"c": 1 - c}
        )

    def product(slot, x_a):
        for zh_a in (0, 1):
            b_a = zh_a * 4 + x_a
            at_zl, at_y = b_a // 2, (b_a % 2) * 2
            for zh_b in (0, 1):
                tile = lax.dot_general(
                    xg[slot, zh_a].reshape(ROWS, BD), xg[0, zh_b].reshape(ROWS, BD), (((0,), (0,)), ((), ())), preferred_element_type=F32
                ).astype(BF)
                for s in range(4):
                    pb[s % 2, at_zl, at_y + s // 2, zh_b] = tile[s * 64 : s * 64 + 64]
            c_copy(b_a).start()

    x_of = [x, (x + 3) % 4, (x + 1) % 4, (x + 2) % 4]
    for slot in range(4):
        if slot == 3:
            for j in range(NCH):
                for h in (0, 1):
                    x_copy(2 if j < NCH // 2 else 3, j, h).wait_recv()
        product(slot, x_of[slot])

    for slot in range(4):
        for zh_a in (0, 1):
            b_a = zh_a * 4 + x_of[slot]
            at_zl, at_y = b_a // 2, pl.ds((b_a % 2) * 2, 2)
            c_copy(b_a).wait_recv()
            s1[at_zl, at_y] = (
                pb[c, at_zl, at_y].astype(F32) + rc[at_zl, at_y].astype(F32)
            ).astype(BF)

    def y_copy(d):
        to = (y + d) % 4
        return remote(s1.at[:, to], ry.at[d - 1], ysend.at[d - 1], yrecv.at[d - 1], {"y": to})

    for d in (2, 1, 3):
        y_copy(d).start()
    for d in (1, 3, 2):
        y_copy(d).wait_recv()
    for k in range(4):
        total = s1[k, y].astype(F32)
        for d in range(3):
            total = total + ry[d, k].astype(F32)
        s2[k] = total.astype(BF)

    def r_copy(d):
        to = (z + d) % 8
        return remote(s2.at[to % 4, to // 4], rz.at[d - 1], rsend.at[d - 1], rrecv.at[d - 1], z_id(to))

    for d in (4, 3, 5, 2, 6, 1, 7):
        r_copy(d).start()
    total = s2[zl, zh].astype(F32)
    for d in (1, 7, 2, 6, 3, 5, 4):
        r_copy(d).wait_recv()
        total = total + rz[d - 1].astype(F32)
    mv[...] = total * (1.0 / 65536.0)
    store_m = pltpu.make_async_copy(mv, out_m, lsem.at[4])
    store_m.start()

    for copy in (up0, down0, up1, down1):
        copy.wait_send()
    for j in range(NCH):
        for half in (0, 1):
            z_copy(half, j, zh).wait_send()
        for h in (0, 1):
            x_copy(0, j, h).wait_send()
            x_copy(1, j, h).wait_send()
            x_copy(2 if j < NCH // 2 else 3, j, h).wait_send()
    for b_a in range(8):
        c_copy(b_a).wait_send()
    for d in (1, 2, 3):
        y_copy(d).wait_send()
    for d in range(1, 8):
        r_copy(d).wait_send()
    store_f.wait()
    store_m.wait()


def on_device(y_current, y_previous, h_blocks, basis_sizes, neighbours):
    tbl = make_tables(neighbours, basis_sizes)
    any_space = pl.BlockSpec(memory_space=pl.ANY)
    dma = pltpu.SemaphoreType.DMA
    return pl.pallas_call(
        main_kernel,
        out_shape=(
            jax.ShapeDtypeStruct((EL, BMAX, BD), BF),
            jax.ShapeDtypeStruct((64, BD), F32),
        ),
        in_specs=[pl.BlockSpec(memory_space=pltpu.SMEM)] + [any_space] * 3,
        out_specs=(any_space, any_space),
        scratch_shapes=[
            pltpu.VMEM((EL, BMAX, BD), BF),
            pltpu.VMEM((EL, BMAX, BD), BF),
            pltpu.VMEM((EL, BMAX, 5 * BMAX), BF),
            pltpu.VMEM((EL, BMAX, BD), BF),
            pltpu.VMEM((EL, BMAX, BD), BF),
            *[pltpu.VMEM((GY, BMAX, BD), BF)] * 4,
            pltpu.VMEM((EL, BMAX, BD), F32),
            pltpu.VMEM((EL, BMAX, BD), BF),
            pltpu.VMEM((EL, BMAX, BD), BF),
            pltpu.VMEM((4, 2, GY, BMAX, BD), BF),
            pltpu.VMEM((2, 4, 4, 2, 64, BD), BF),
            pltpu.VMEM((4, 4, 2, 64, BD), BF),
            pltpu.VMEM((4, 4, 2, 64, BD), BF),
            pltpu.VMEM((3, 4, 2, 64, BD), BF),
            pltpu.VMEM((4, 2, 64, BD), BF),
            pltpu.VMEM((7, 64, BD), BF),
            pltpu.VMEM((64, BD), F32),
            dma((5,)),
            dma((2, 2)), dma((2, 2)),
            dma((2, NCH)), dma((2, NCH)),
            dma((3, NCH, 2)), dma((3, NCH, 2)),
            dma((8,)), dma((8,)),
            dma((3,)), dma((3,)),
            dma((7,)), dma((7,)),
        ],
        compiler_params=pltpu.CompilerParams(collective_id=0, has_side_effects=True),
    )(tbl, y_current, y_previous, h_blocks)


def solution(mesh):
    split = Mesh(mesh.devices.reshape(4, 4, 2, 2, 4), ELEM + BAND)
    return jax.shard_map(
        on_device,
        mesh=split,
        in_specs=(
            P(ELEM, None, BAND),
            P(ELEM, None, BAND),
            P(ELEM, None, None),
            P(ELEM),
            P(ELEM, None),
        ),
        out_specs=(P(ELEM, None, BAND), P(ELEM, BAND)),
        check_vma=False,
    )
```

time: 265 us -> 113 us (0.43)
  the two profiles are of different devices: /device:TPU:2 before, /device:TPU:38 now
where the time goes in v1:
time: 113 us
  Pallas kernels  108 us (96%)
  local copies, waits for them, and re-layouts  4.34 us (4%)
    pallas_call x1, Pallas kernels, on_device(): pl.pallas_call(main_kernel, out_shape=(jax.ShapeDtypeStruct((EL, BMAX, BD...  105 us
    unnamed x5, local copies, waits for them, and re-layouts  4.34 us
    pallas_call x1, Pallas kernels, make_tables(): pl.pallas_call(tables_kernel, out_shape=jax.ShapeDtypeStruct((EL, 8), jnp...  3.62 us

profile of v1, /device:TPU:38, one launch (start us, length us, event | category | flops | bytes accessed | tf_op | source)
XLA Modules:
  0.0 113.2 jit_solution(13872766980532777750)
XLA Ops:
  0.6 1.4 %copy.7.nb = s32[32,4]{1,0:T(8,128)} copy(s32[32,4]{0,1:T(4,128)} %param.9) | data formatting | bytes 1024 | tf_op args[4]
  2.0 3.6 %shard_map.68.tbl = s32[32,8]{1,0:T(8,128)} custom-call(s32[32,4]{1,0:T(8,128)} %copy.7.nb, s32[32]{0:T(128)} %sizes.1), custom_call_target="tpu_custom_call" | custom-call | tf_op jit(solution)/shard_map/pallas_call | solution.py:69
  5.6 104.6 %shard_map.69 = (bf16[32,64,256]{2,1,0:T(8,128)(2,1)}, f32[64,256]{1,0:T(8,128)}) custom-call(s32[32,8]{1,0:T(8,128)} %shard_map.68.tbl, bf16[32,64,256]{2,1,0:T(8,128)(2,1)} %yc_h.1, bf16[32,64,256]{2,1,0:T(8,128)(2,1)} %yp_h.1, bf16[32,64,320]{2,1,0:T(8,128)(2,1)} %h_h.1), custom_call_target="tpu_custom_call" | custom-call | tf_op jit(solution)/shard_map/pallas_call | solution.py:327
  110.2 0.0 copy-start
  110.2 2.3 %copy.10 = bf16[32,64,256]{2,1,0:T(8,128)(2,1)} copy(bf16[32,64,256]{2,1,0:T(8,128)(2,1)} %get-tuple-element.4) | data formatting | bytes 2097152
  112.6 0.0 copy-done
  112.6 0.6 copy.11
Async XLA Ops:
  110.2 2.3 %copy-start = (f32[64,256]{1,0:T(8,128)S(1)}, f32[64,256]{1,0:T(8,128)}, u32[]{:S(2)}) copy-start(f32[64,256]{1,0:T(8,128)} %get-tuple-element.5) | copy-start | bytes 196612

commit v2 on v1

v2 whole, which is shorter than its diff:
```python
import jax
import jax.numpy as jnp
from jax import lax
from jax.experimental import pallas as pl
from jax.experimental.pallas import tpu as pltpu
from jax.sharding import Mesh
from jax.sharding import PartitionSpec as P

BMAX = 64
EL = 32
GY = 16
BD = 256
NB = 2048
ROWS = GY * BMAX
CH = 2
NCH = GY // CH
HALF = NCH // 2

CENTER = 0.3
SCALE = 2.0 / 1.7

ELEM = ("zl", "y", "c")
BAND = ("zh", "x")
BF = jnp.bfloat16
F32 = jnp.float32
MESH_ID = pl.DeviceIdType.MESH


def tables_kernel(nb, sizes, tbl, slot, mark, rank):
    me = (lax.axis_index("zl") * 4 + lax.axis_index("y")) * 2 + lax.axis_index("c")
    for i in range(2 * EL):
        mark[i] = 0
    ones = jnp.int32(0)
    rows = []
    for i in range(EL):
        row = jnp.where(nb[0, i] >> 5 == me, 1, 0)
        at = jnp.where(row == 1, GY + ones, i - ones)
        slot[i] = at
        tbl[at, 0] = i
        tbl[at, 1] = sizes[i]
        tbl[i, 6] = at
        mark[row * EL + (nb[row, i] & (EL - 1))] = 1
        ones = ones + row
        rows.append(row)
    seen = jnp.int32(0)
    for i in range(2 * EL):
        rank[i] = seen
        seen = seen + mark[i]
    for i in range(EL):
        at, row = slot[i], rows[i]
        tbl[at, 2] = slot[nb[1 - row, i] & (EL - 1)]
        tbl[at, 3] = slot[nb[2, i] & (EL - 1)]
        tbl[at, 4] = slot[nb[3, i] & (EL - 1)]
        tbl[at, 5] = rank[row * EL + (nb[row, i] & (EL - 1))] - row * GY


def make_tables(neighbours, basis_sizes):
    smem = pl.BlockSpec(memory_space=pltpu.SMEM)
    return pl.pallas_call(
        tables_kernel,
        out_shape=jax.ShapeDtypeStruct((EL, 8), jnp.int32),
        in_specs=[smem, smem],
        out_specs=smem,
        scratch_shapes=[
            pltpu.SMEM((EL,), jnp.int32),
            pltpu.SMEM((2 * EL,), jnp.int32),
            pltpu.SMEM((2 * EL,), jnp.int32),
        ],
        name="tables",
    )(neighbours.T, basis_sizes)


def main_kernel(
    tbl_h, yc_h, yp_h, h_h, out_f, out_m, tbl,
    yc, yp, hv, cur0, cur1, far_p0, far_n0, far_p1, far_n1, acc, fil, outv, xg, x1, x2, x3, pb, rc, s1, ry, s2, rz, mv, ft, fr,
    lsem, hsend, hrecv, zsend, zrecv, xsend, xrecv, gsend, grecv, csend, crecv, ysend, yrecv, rsend, rrecv, fsend, frecv,
):
    zl, y, c = (lax.axis_index(a) for a in ELEM)
    zh, x = (lax.axis_index(a) for a in BAND)
    z = zh * 4 + zl
    e = (zl * 4 + y) * 2 + c

    def elem_id(other):
        return {"zl": other // 8, "y": (other // 2) % 4, "c": other % 2}

    def z_id(other):
        return {"zh": other // 4, "zl": other % 4}

    nxt, prv = elem_id((e + 1) % 32), elem_id((e + 31) % 32)
    xp, xm = {"x": (x + 1) % 4}, {"x": (x + 3) % 4}

    def remote(src, dst, ss, rs, to):
        return pltpu.make_async_remote_copy(
            src_ref=src, dst_ref=dst, send_sem=ss, recv_sem=rs, device_id=to, device_id_type=MESH_ID
        )

    load_t = pltpu.make_async_copy(tbl_h, tbl, lsem.at[5])
    load_c = pltpu.make_async_copy(yc_h, yc, lsem.at[0])
    load_p = pltpu.make_async_copy(yp_h, yp, lsem.at[1])
    load_h = pltpu.make_async_copy(h_h, hv, lsem.at[2])
    load_t.start()
    load_c.start()
    load_h.start()
    load_p.start()

    barrier = pltpu.get_barrier_semaphore()
    partners = [nxt, prv, xp, xm]
    partners += [{"y": (y + d) % 4} for d in (1, 2, 3)]
    partners += [z_id((z + d) % 8) for d in range(1, 8)]
    for to in partners:
        pl.semaphore_signal(barrier, inc=1, device_id=to, device_id_type=MESH_ID)

    b_own, b_rows, s_rows = zh * 4 + x, e // 4, e % 4
    mirrored = b_rows % 4 != x

    def mirror_id(s):
        return {**elem_id(4 * b_own + s), "zh": b_rows // 4, "x": b_rows % 4}

    @pl.when(mirrored)
    def _():
        for s in range(4):
            pl.semaphore_signal(barrier, inc=1, device_id=mirror_id(s), device_id_type=MESH_ID)


    rows = lax.broadcasted_iota(jnp.int32, (BMAX, BD), 0)
    zero = jnp.zeros((BMAX, BD), BF)

    with jax.named_scope('w_load'):
        load_t.wait()
        load_c.wait()

    def pack(p, _):
        value = yc[tbl[p, 0]].astype(F32)
        cur0[p] = jnp.where(rows < tbl[p, 1], value, 0.0).astype(BF)
        return 0

    with jax.named_scope('pack1'):
        lax.fori_loop(GY, EL, pack, 0, unroll=4)
    with jax.named_scope('barrier'):
        pl.semaphore_wait(barrier, len(partners) + 4 * mirrored.astype(jnp.int32))

    halo = ((far_p0, far_n0), (far_p1, far_n1))

    def halo_copies(cur, degree):
        up = remote(cur.at[pl.ds(GY, GY)], halo[degree][0], hsend.at[degree, 0], hrecv.at[degree, 0], nxt)
        down = remote(cur.at[pl.ds(0, GY)], halo[degree][1], hsend.at[degree, 1], hrecv.at[degree, 1], prv)
        return up, down

    up0, down0 = halo_copies(cur0, 0)
    up0.start()
    with jax.named_scope('pack0'):
        lax.fori_loop(0, GY, pack, 0, unroll=4)
    down0.start()
    load_h.wait()
    load_p.wait()

    def local_part(cur, prev_of, row):
        def one(p, _):
            i = tbl[p, 0]
            own, n2, n3, n4 = cur[p], cur[tbl[p, 2]], cur[tbl[p, 3]], cur[tbl[p, 4]]
            pair = [zero, n2] if row == 0 else [n2, zero]
            stack = jnp.concatenate([own] + pair + [n3, n4], axis=0)
            applied = jnp.dot(hv[i], stack, preferred_element_type=F32)
            acc[p] = SCALE * (applied - CENTER * own.astype(F32)) - prev_of(p, i).astype(F32)
            return 0

        lax.fori_loop(row * GY, row * GY + GY, one, 0, unroll=8)

    def full_value(p, row, degree):
        i = tbl[p, 0]
        far = halo[degree][row][tbl[p, 5]]
        if row == 0:
            applied = jnp.dot(hv[i, :, 0:128], jnp.concatenate([zero, far], axis=0), preferred_element_type=F32)
        else:
            applied = jnp.dot(hv[i, :, 128:256], jnp.concatenate([far, zero], axis=0), preferred_element_type=F32)
        return jnp.where(rows < tbl[p, 1], acc[p] + SCALE * applied, 0.0).astype(BF)

    with jax.named_scope('local0'):
      for row in (1, 0):
        local_part(cur0, lambda p, i: yp[i], row)

    up1, down1 = halo_copies(cur1, 1)

    def first(row):
        def one(p, _):
            cur1[p] = full_value(p, row, 0)
            return 0

        lax.fori_loop(row * GY, row * GY + GY, one, 0, unroll=8)

    with jax.named_scope('w_halo0'):
        down0.wait_recv()
    with jax.named_scope('first1'):
        first(1)
    up1.start()
    with jax.named_scope('w_halo0b'):
        up0.wait_recv()
    with jax.named_scope('first0'):
        first(0)
    down1.start()

    with jax.named_scope('local1'):
      for row in (1, 0):
        local_part(cur1, lambda p, i: cur0[p], row)
    with jax.named_scope('w_halo1'):
        down1.wait_recv()
        up1.wait_recv()

    def swap(front, k):
        return 2 * (front + (k // 2) * (1 - 2 * front)) + k % 2

    def piece(k, front):
        return (k % 2) * HALF + swap(front, k // 2)

    to_pass = ((x + 2) % 4) // 2

    def z_copy(half, k, src_zh):
        j = piece(k, to_pass)
        return remote(
            fil.at[pl.ds(half * GY + j * CH, CH)], xg.at[src_zh, pl.ds(j * CH, CH)],
            zsend.at[half, k], zrecv.at[src_zh, k], z_id((zl + 2 + 4 * half) % 8),
        )

    def second(kk, _):
        for k in (2 * kk, 2 * kk + 1):
            for row in (1, 0):
                for m in range(CH):
                    p = row * GY + piece(k, to_pass) * CH + m
                    fil[p] = full_value(p, row, 1)
        for k in (2 * kk, 2 * kk + 1):
            for row in (1, 0):
                z_copy(row, k, zh).start()
        return 0

    with jax.named_scope('second'):
        lax.fori_loop(0, HALF, second, 0)

    def put(i, _):
        s = tbl[i, 6]
        outv[i] = fil[s]
        return 0

    with jax.named_scope('put'):
        lax.fori_loop(0, EL, put, 0, unroll=4)
    store_f = pltpu.make_async_copy(outv, out_f, lsem.at[3])
    store_f.start()

    def x_copy(way, q, h, front):
        at = swap(front, q) * CH
        return remote(
            xg.at[h, pl.ds(way * HALF * CH + at, CH)], (x1, x2)[way].at[h, pl.ds(at, CH)],
            xsend.at[way, q, h], xrecv.at[way, q, h], (xp, xm)[way],
        )

    came = (((x + 1) % 4) // 2, ((x + 3) % 4) // 2)

    def pass_on(way, q, h):
        at = swap(came[way], q) * CH
        return remote(
            (x1, x2)[way].at[h, pl.ds(at, CH)], x3.at[h, way, pl.ds(q * CH, CH)],
            gsend.at[way, q, h], grecv.at[way, q, h], (xp, xm)[way],
        )

    for k in range(NCH):
        way, q = k % 2, k // 2
        for h in (0, 1):
            with jax.named_scope(f'wz{k}{h}'):
                z_copy(0, k, h).wait_recv()
            x_copy(way, q, h, to_pass).start()
        if 2 <= k < 6:
            way, q = k % 2, k // 2 - 1
            for h in (0, 1):
                with jax.named_scope(f'wx{k}{h}'):
                    x_copy(way, q, h, came[way]).wait_recv()
                pass_on(way, q, h).start()

    def c_copy(b_a):
        at_zl, at_y = b_a // 2, pl.ds((b_a % 2) * 2, 2)
        return remote(
            pb.at[1 - c, at_zl, at_y], rc.at[at_zl, at_y], csend.at[b_a], crecv.at[b_a], {"c": 1 - c}
        )

    def product(x_a, left, right):
        for zh_a in (0, 1):
            b_a = zh_a * 4 + x_a
            at_zl, at_y = b_a // 2, (b_a % 2) * 2
            for zh_b in (0, 1):
                tile = lax.dot_general(
                    left(zh_a).reshape(-1, BD), right(zh_b).reshape(-1, BD), (((0,), (0,)), ((), ())),
                    preferred_element_type=F32,
                ).astype(BF)
                for s in range(4):
                    pb[s % 2, at_zl, at_y + s // 2, zh_b] = tile[s * 64 : s * 64 + 64]
            c_copy(b_a).start()

    def settle(x_a):
        for zh_a in (0, 1):
            b_a = zh_a * 4 + x_a
            at_zl, at_y = b_a // 2, pl.ds((b_a % 2) * 2, 2)
            with jax.named_scope(f'wc{zh_a}'):
                c_copy(b_a).wait_recv()
            s1[at_zl, at_y] = (
                pb[c, at_zl, at_y].astype(F32) + rc[at_zl, at_y].astype(F32)
            ).astype(BF)

    def y_copy(to, d):
        return remote(s1.at[:, to], ry.at[d - 1], ysend.at[d - 1], yrecv.at[d - 1], {"y": to})

    def y_start(parity):
        for k in (0, 1):
            to = parity * 2 + k

            @pl.when(to != y)
            def _():
                y_copy(to, (to + 4 - y) % 4).start()

    quarter = (x // 2) * GY // 4
    x_far, x_prev, x_next = (x + 2) % 4, (x + 3) % 4, (x + 1) % 4

    with jax.named_scope('prod_own'):
        product(x, lambda h: xg[h], lambda h: xg[h])
    with jax.named_scope('w_pass'):
        for way in (0, 1):
            for q in (0, 1):
                for h in (0, 1):
                    pass_on(way, q, h).wait_recv()
    with jax.named_scope('prod_far'):
        product(
            x_far, lambda h: x3[h],
            lambda h: jnp.concatenate([xg[h, pl.ds(quarter, 4)], xg[h, pl.ds(GY // 2 + quarter, 4)]], axis=0),
        )
    settle(x)
    settle(x_far)
    y_start(x % 2)
    for way in (0, 1):
        with jax.named_scope(f'w_x{way}'):
            for q in (2, 3):
                for h in (0, 1):
                    x_copy(way, q, h, came[way]).wait_recv()
        part = pl.ds(way * GY // 2, GY // 2)
        with jax.named_scope(f'prod_x{way}'):
            product((x_prev, x_next)[way], lambda h: (x1, x2)[way][h], lambda h: xg[h, part])
    settle(x_prev)
    settle(x_next)
    y_start(1 - x % 2)

    for d in (1, 3, 2):
        with jax.named_scope(f'wy{d}'):
            y_copy((y + d) % 4, d).wait_recv()
    for k in range(4):
        total = s1[k, y].astype(F32)
        for d in range(3):
            total = total + ry[d, k].astype(F32)
        s2[k] = total.astype(BF)

    def r_copy(d):
        to = (z + d) % 8
        return remote(s2.at[to % 4, to // 4], rz.at[d - 1], rsend.at[d - 1], rrecv.at[d - 1], z_id(to))

    for d in (4, 3, 5, 2, 6, 1, 7):
        r_copy(d).start()
    total = s2[zl, zh].astype(F32)
    for d in (1, 7, 2, 6, 3, 5, 4):
        with jax.named_scope(f'wr{d}'):
            r_copy(d).wait_recv()
        total = total + rz[d - 1].astype(F32)
    total = total * (1.0 / 65536.0)
    mv[...] = total

    def f_copy(s, recv):
        return remote(ft.at[s], fr.at[recv], fsend.at[s], frecv.at[recv], mirror_id(s))

    @pl.when(mirrored)
    def _():
        turned = total.T.astype(BF)
        for s in range(4):
            ft[s] = turned[s * 64 : s * 64 + 64]
            f_copy(s, s_rows).start()
        with jax.named_scope('w_mirror'):
            for s in range(4):
                f_copy(s, s).wait_recv()
        mv[...] = mv[...] + jnp.concatenate([fr[s].astype(F32) for s in range(4)], axis=1)
        for s in range(4):
            f_copy(s, s_rows).wait_send()

    store_m = pltpu.make_async_copy(mv, out_m, lsem.at[4])
    store_m.start()

    with jax.named_scope('tail'):
      for copy in (up0, down0, up1, down1):
        copy.wait_send()
    for k in range(NCH):
        for h in (0, 1):
            z_copy(h, k, zh).wait_send()
            x_copy(k % 2, k // 2, h, to_pass).wait_send()
    for way in (0, 1):
        for q in (0, 1):
            for h in (0, 1):
                pass_on(way, q, h).wait_send()
    for b_a in range(8):
        c_copy(b_a).wait_send()
    for d in (1, 2, 3):
        y_copy((y + d) % 4, d).wait_send()
    for d in range(1, 8):
        r_copy(d).wait_send()
    store_f.wait()
    store_m.wait()


def on_device(y_current, y_previous, h_blocks, basis_sizes, neighbours):
    tbl = make_tables(neighbours, basis_sizes)
    any_space = pl.BlockSpec(memory_space=pl.ANY)
    dma = pltpu.SemaphoreType.DMA
    return pl.pallas_call(
        main_kernel,
        out_shape=(
            jax.ShapeDtypeStruct((EL, BMAX, BD), BF),
            jax.ShapeDtypeStruct((64, BD), F32),
        ),
        in_specs=[any_space] * 4,
        out_specs=(any_space, any_space),
        scratch_shapes=[
            pltpu.SMEM((EL, 8), jnp.int32),
            pltpu.VMEM((EL, BMAX, BD), BF),
            pltpu.VMEM((EL, BMAX, BD), BF),
            pltpu.VMEM((EL, BMAX, 5 * BMAX), BF),
            pltpu.VMEM((EL, BMAX, BD), BF),
            pltpu.VMEM((EL, BMAX, BD), BF),
            *[pltpu.VMEM((GY, BMAX, BD), BF)] * 4,
            pltpu.VMEM((EL, BMAX, BD), F32),
            pltpu.VMEM((EL, BMAX, BD), BF),
            pltpu.VMEM((EL, BMAX, BD), BF),
            pltpu.VMEM((2, GY, BMAX, BD), BF),
            pltpu.VMEM((2, GY // 2, BMAX, BD), BF),
            pltpu.VMEM((2, GY // 2, BMAX, BD), BF),
            pltpu.VMEM((2, 2, GY // 4, BMAX, BD), BF),
            pltpu.VMEM((2, 4, 4, 2, 64, BD), BF),
            pltpu.VMEM((4, 4, 2, 64, BD), BF),
            pltpu.VMEM((4, 4, 2, 64, BD), BF),
            pltpu.VMEM((3, 4, 2, 64, BD), BF),
            pltpu.VMEM((4, 2, 64, BD), BF),
            pltpu.VMEM((7, 64, BD), BF),
            pltpu.VMEM((64, BD), F32),
            pltpu.VMEM((4, 64, 64), BF),
            pltpu.VMEM((4, 64, 64), BF),
            dma((6,)),
            dma((2, 2)), dma((2, 2)),
            dma((2, NCH)), dma((2, NCH)),
            dma((2, HALF, 2)), dma((2, HALF, 2)),
            dma((2, 2, 2)), dma((2, 2, 2)),
            dma((8,)), dma((8,)),
            dma((3,)), dma((3,)),
            dma((7,)), dma((7,)),
            dma((4,)), dma((4,)),
        ],
        compiler_params=pltpu.CompilerParams(collective_id=0, has_side_effects=True),
        name="chain",
    )(tbl, y_current, y_previous, h_blocks)


def solution(mesh):
    split = Mesh(mesh.devices.reshape(4, 4, 2, 2, 4), ELEM + BAND)
    return jax.shard_map(
        on_device,
        mesh=split,
        in_specs=(
            P(ELEM, None, BAND),
            P(ELEM, None, BAND),
            P(ELEM, None, None),
            P(ELEM),
            P(ELEM, None),
        ),
        out_specs=(P(ELEM, None, BAND), P(ELEM, BAND)),
        check_vma=False,
    )
```

time: 113 us -> 96.9 us (0.86)
  the two profiles are of different devices: /device:TPU:38 before, /device:TPU:57 now
where the time goes in v2:
time: 96.9 us; the launch traced here: 96.7 us
  Pallas kernels  93.1 us (96%)
  local copies, waits for them, and re-layouts  2.97 us (3%)
    pallas_call x1, Pallas kernels, on_device(): pl.pallas_call(main_kernel, out_shape=(jax.ShapeDtypeStruct((EL, BMAX, BD...  91.1 us
    unnamed x4, local copies, waits for them, and re-layouts  2.97 us
    pallas_call x1, Pallas kernels, make_tables(): pl.pallas_call(tables_kernel, out_shape=jax.ShapeDtypeStruct((EL, 8), jnp...  2.07 us

profile of v2, /device:TPU:57, one launch (start us, length us, event | category | flops | bytes accessed | tf_op | source)
XLA Modules:
  0.0 96.7 jit_solution(14454690052274138887)
XLA Ops:
  0.6 2.1 %tables.1.tbl_h = s32[32,8]{1,0:T(8,128)} custom-call(s32[4,32]{1,0:T(4,128)} %bitcast.1, s32[32]{0:T(128)} %sizes.1), custom_call_target="tpu_custom_call" | custom-call | tf_op jit(solution)/shard_map/tables/pallas_call | solution.py:59
  2.7 91.1 %chain.1 = (bf16[32,64,256]{2,1,0:T(8,128)(2,1)}, f32[64,256]{1,0:T(8,128)}) custom-call(s32[32,8]{1,0:T(8,128)} %tables.1.tbl_h, bf16[32,64,256]{2,1,0:T(8,128)(2,1)} %yc_h.1, bf16[32,64,256]{2,1,0:T(8,128)(2,1)} %yp_h.1, bf16[32,64,320]{2,1,0:T(8,128)(2,1)} %h_h.1), custom_call_target="tpu_custom_call" | custom-call | tf_op jit(solution)/shard_map/chain/pallas_call | solution.py:414
  93.8 0.0 copy-start
  93.8 2.3 %copy.9 = bf16[32,64,256]{2,1,0:T(8,128)(2,1)} copy(bf16[32,64,256]{2,1,0:T(8,128)(2,1)} %get-tuple-element.4) | data formatting | bytes 2097152
  96.1 0.0 copy-done
  96.1 0.6 copy.10
Async XLA Ops:
  93.8 2.3 %copy-start = (f32[64,256]{1,0:T(8,128)S(1)}, f32[64,256]{1,0:T(8,128)}, u32[]{:S(2)}) copy-start(f32[64,256]{1,0:T(8,128)} %get-tuple-element.5) | copy-start | bytes 196612

commit v3 on v2

v3 whole, which is shorter than its diff:
```python
import jax
import jax.numpy as jnp
from jax import lax
from jax.experimental import pallas as pl
from jax.experimental.pallas import tpu as pltpu
from jax.sharding import Mesh
from jax.sharding import PartitionSpec as P

BMAX = 64
EL = 32
GY = 16
BD = 256
NB = 2048
ROWS = GY * BMAX
HB = 128
CH = 4
NCH = GY // CH
ORDER = (0, 2, 1, 3)

CENTER = 0.3
SCALE = 2.0 / 1.7

ELEM = ("zl", "y", "c")
BAND = ("zh", "x")
BF = jnp.bfloat16
F32 = jnp.float32
MESH_ID = pl.DeviceIdType.MESH


def tables_kernel(nb, sizes, tbl, slot, mark, rank):
    me = (lax.axis_index("zl") * 4 + lax.axis_index("y")) * 2 + lax.axis_index("c")
    for i in range(2 * EL):
        mark[i] = 0
    ones = jnp.int32(0)
    rows = []
    for i in range(EL):
        row = jnp.where(nb[0, i] >> 5 == me, 1, 0)
        at = jnp.where(row == 1, GY + ones, i - ones)
        slot[i] = at
        tbl[at, 0] = i
        tbl[at, 1] = sizes[i]
        tbl[i, 6] = at
        mark[row * EL + (nb[row, i] & (EL - 1))] = 1
        ones = ones + row
        rows.append(row)
    seen = jnp.int32(0)
    for i in range(2 * EL):
        rank[i] = seen
        seen = seen + mark[i]
    for i in range(EL):
        at, row = slot[i], rows[i]
        tbl[at, 2] = slot[nb[1 - row, i] & (EL - 1)]
        tbl[at, 3] = slot[nb[2, i] & (EL - 1)]
        tbl[at, 4] = slot[nb[3, i] & (EL - 1)]
        tbl[at, 5] = rank[row * EL + (nb[row, i] & (EL - 1))] - row * GY


def make_tables(neighbours, basis_sizes):
    smem = pl.BlockSpec(memory_space=pltpu.SMEM)
    return pl.pallas_call(
        tables_kernel,
        out_shape=jax.ShapeDtypeStruct((EL, 8), jnp.int32),
        in_specs=[smem, smem],
        out_specs=smem,
        scratch_shapes=[
            pltpu.SMEM((EL,), jnp.int32),
            pltpu.SMEM((2 * EL,), jnp.int32),
            pltpu.SMEM((2 * EL,), jnp.int32),
        ],
        name="tables",
    )(neighbours.T, basis_sizes)


def main_kernel(
    tbl_h, yc_h, yp_h, h_h, out_f, out_m, tbl,
    yc, yp, hv, cur0, cur1, f000, f001, f010, f011, f100, f101, f110, f111,
    acc, fil, outv, xg, x1, x2, x3, pb, rc, s1, ry, s2, rz, mv,
    lsem, hsend, hrecv, zsend, zrecv, xsend, xrecv, gsend, grecv, csend, crecv, ysend, yrecv, rsend, rrecv,
):
    zl, y, c = (lax.axis_index(a) for a in ELEM)
    zh, x = (lax.axis_index(a) for a in BAND)
    z = zh * 4 + zl
    e = (zl * 4 + y) * 2 + c

    def elem_id(other):
        return {"zl": other // 8, "y": (other // 2) % 4, "c": other % 2}

    def z_id(other):
        return {"zh": other // 4, "zl": other % 4}

    nxt, prv = elem_id((e + 1) % 32), elem_id((e + 31) % 32)
    x_prev, x_next, x_far = (x + 3) % 4, (x + 1) % 4, (x + 2) % 4
    xp, xm = {"x": x_next}, {"x": x_prev}

    def remote(src, dst, ss, rs, to):
        return pltpu.make_async_remote_copy(
            src_ref=src, dst_ref=dst, send_sem=ss, recv_sem=rs, device_id=to, device_id_type=MESH_ID
        )

    loads = [
        pltpu.make_async_copy(src, dst, lsem.at[k])
        for k, (src, dst) in enumerate(
            [(tbl_h, tbl)]
            + [(yc_h.at[:, :, pl.ds(b * HB, HB)], yc.at[b]) for b in (0, 1)]
            + [(h_h, hv)]
            + [(yp_h.at[:, :, pl.ds(b * HB, HB)], yp.at[b]) for b in (0, 1)]
        )
    ]
    for load in loads:
        load.start()

    barrier = pltpu.get_barrier_semaphore()
    partners = [nxt, prv, xp, xm]
    partners += [{"y": (y + d) % 4} for d in (1, 2, 3)]
    partners += [z_id((z + d) % 8) for d in range(1, 8)]
    for to in partners:
        pl.semaphore_signal(barrier, inc=1, device_id=to, device_id_type=MESH_ID)

    rows = lax.broadcasted_iota(jnp.int32, (BMAX, HB), 0)
    zero = jnp.zeros((BMAX, HB), BF)

    with jax.named_scope('w_load'):
        for load in loads[:3]:
            load.wait()

    def pack(row, b):
        def one(p, _):
            value = yc[b, tbl[p, 0]].astype(F32)
            cur0[b, p] = jnp.where(rows < tbl[p, 1], value, 0.0).astype(BF)
            return 0

        lax.fori_loop(row * GY, row * GY + GY, one, 0, unroll=4)

    halo = (((f000, f001), (f010, f011)), ((f100, f101), (f110, f111)))

    def halo_copy(degree, row, b):
        return remote(
            (cur0, cur1)[degree].at[b, pl.ds((1 - row) * GY, GY)], halo[degree][row][b],
            hsend.at[degree, row, b], hrecv.at[degree, row, b], (nxt, prv)[row],
        )

    with jax.named_scope('pack'):
        pack(1, 0)
    with jax.named_scope('barrier'):
        pl.semaphore_wait(barrier, len(partners))
    halo_copy(0, 0, 0).start()
    pack(0, 0)
    halo_copy(0, 1, 0).start()
    pack(1, 1)
    halo_copy(0, 0, 1).start()
    pack(0, 1)
    halo_copy(0, 1, 1).start()
    for load in loads[3:]:
        load.wait()

    def local_part(degree, row, b):
        cur = (cur0, cur1)[degree]

        def one(p, _):
            i = tbl[p, 0]
            own, n2, n3, n4 = cur[b, p], cur[b, tbl[p, 2]], cur[b, tbl[p, 3]], cur[b, tbl[p, 4]]
            pair = [zero, n2] if row == 0 else [n2, zero]
            stack = jnp.concatenate([own] + pair + [n3, n4], axis=0)
            applied = jnp.dot(hv[i], stack, preferred_element_type=F32)
            before = yp[b, i] if degree == 0 else cur0[b, p]
            acc[b, p] = SCALE * (applied - CENTER * own.astype(F32)) - before.astype(F32)
            return 0

        lax.fori_loop(row * GY, row * GY + GY, one, 0, unroll=8)

    def full_value(degree, row, b, p):
        i = tbl[p, 0]
        far = halo[degree][row][b][tbl[p, 5]]
        if row == 0:
            applied = jnp.dot(hv[i, :, 0:128], jnp.concatenate([zero, far], axis=0), preferred_element_type=F32)
        else:
            applied = jnp.dot(hv[i, :, 128:256], jnp.concatenate([far, zero], axis=0), preferred_element_type=F32)
        return jnp.where(rows < tbl[p, 1], acc[b, p] + SCALE * applied, 0.0).astype(BF)

    def first(row, b):
        def one(p, _):
            cur1[b, p] = full_value(0, row, b, p)
            return 0

        lax.fori_loop(row * GY, row * GY + GY, one, 0, unroll=8)

    def z_copy(half, b, j, src_zh):
        return remote(
            fil.at[b, pl.ds(half * GY + j * CH, CH)], xg.at[b, src_zh, pl.ds(j * CH, CH)],
            zsend.at[half, b, j], zrecv.at[src_zh, b, j], z_id((zl + 2 + 4 * half) % 8),
        )

    def second(b):
        def one(k, _):
            j = (k % 2) * 2 + k // 2
            for row in (1, 0):
                for m in range(CH):
                    p = row * GY + j * CH + m
                    fil[b, p] = full_value(1, row, b, p)
            for row in (1, 0):
                z_copy(row, b, j, zh).start()
            return 0

        lax.fori_loop(0, NCH, one, 0)

    for b in (0, 1):
        with jax.named_scope(f'local0{b}'):
            local_part(0, 1, b)
            local_part(0, 0, b)
    for b in (0, 1):
        with jax.named_scope(f'w_h0{b}1'):
            halo_copy(0, 1, b).wait_recv()
        first(1, b)
        halo_copy(1, 0, b).start()
        with jax.named_scope(f'w_h0{b}0'):
            halo_copy(0, 0, b).wait_recv()
        first(0, b)
        halo_copy(1, 1, b).start()
        with jax.named_scope(f'local1{b}'):
            local_part(1, 1, b)
            local_part(1, 0, b)
    for b in (0, 1):
        with jax.named_scope(f'w_h1{b}'):
            halo_copy(1, 1, b).wait_recv()
            halo_copy(1, 0, b).wait_recv()
        with jax.named_scope(f'second{b}'):
            second(b)

    def put(i, _):
        s = tbl[i, 6]
        outv[i] = jnp.concatenate([fil[0, s], fil[1, s]], axis=1)
        return 0

    with jax.named_scope('put'):
        lax.fori_loop(0, EL, put, 0, unroll=4)
    store_f = pltpu.make_async_copy(outv, out_f, lsem.at[6])
    store_f.start()

    def x_copy(way, b, j, h):
        part = pl.ds(j * CH, CH)
        return remote(
            xg.at[b, h, part], (x1, x2)[way].at[b, h, part],
            xsend.at[way, b, j, h], xrecv.at[way, b, j, h], (xp, xm)[way],
        )

    def pass_on(b, j, h):
        part, way = pl.ds(j * CH, CH), j // 2
        return remote(
            (x1, x2)[way].at[b, h, part], x3.at[b, h, part], gsend.at[b, j, h], grecv.at[b, j, h], (xp, xm)[way]
        )

    for b in (0, 1):
        for j in ORDER:
            for h in (0, 1):
                with jax.named_scope(f'wz{b}{j}{h}'):
                    z_copy(0, b, j, h).wait_recv()
                x_copy(0, b, j, h).start()
                x_copy(1, b, j, h).start()

    def pass_half(b):
        for j in ORDER:
            for h in (0, 1):
                with jax.named_scope(f'wx{b}{j}{h}'):
                    x_copy(j // 2, b, j, h).wait_recv()
                pass_on(b, j, h).start()

    def c_copy(x_a, zh_a):
        at = (zh_a, x_a // 2, pl.ds((x_a % 2) * 2, 2))
        return remote(pb.at[(1 - c, *at)], rc.at[at], csend.at[x_a, zh_a], crecv.at[x_a, zh_a], {"c": 1 - c})

    def whole(ref, h):
        return jnp.concatenate([ref[b, h].reshape(GY * BMAX, HB) for b in (0, 1)], axis=1)

    def product(x_a, ref):
        for zh_a in (0, 1):
            for zh_b in (0, 1):
                tile = lax.dot_general(
                    whole(ref, zh_a), whole(xg, zh_b), (((0,), (0,)), ((), ())), preferred_element_type=F32
                ).astype(BF)
                for s in range(4):
                    pb[s % 2, zh_a, x_a // 2, (x_a % 2) * 2 + s // 2, zh_b] = tile[s * 64 : s * 64 + 64]
            c_copy(x_a, zh_a).start()

    def y_copy(to, d, xh):
        return remote(
            s1.at[:, xh, to], ry.at[d - 1, xh], ysend.at[d - 1, xh], yrecv.at[d - 1, xh], {"y": to}
        )

    def settle(x_a):
        xh, pair = x_a // 2, pl.ds((x_a % 2) * 2, 2)
        for zh_a in (0, 1):
            with jax.named_scope(f'wc{zh_a}'):
                c_copy(x_a, zh_a).wait_recv()
            s1[zh_a, xh, pair] = (
                pb[c, zh_a, xh, pair].astype(F32) + rc[zh_a, xh, pair].astype(F32)
            ).astype(BF)
        for k in (0, 1):
            to = (x_a % 2) * 2 + k

            @pl.when(to != y)
            def _():
                y_copy(to, (to + 4 - y) % 4, xh).start()

    def r_copy(to, src_xh):
        d = (to + 8 - z) % 8
        return remote(
            s2.at[src_xh, (to % 4) // 2, to // 4], rz.at[d - 1], rsend.at[d - 1], rrecv.at[d - 1], z_id(to)
        )

    def gather_y(xh):
        for d in (1, 3, 2):
            y_copy((y + d) % 4, d, xh).wait_recv()
        for zh_a in (0, 1):
            total = s1[zh_a, xh, y].astype(F32)
            for d in range(3):
                total = total + ry[d, xh, zh_a].astype(F32)
            s2[xh, zh_a] = total.astype(BF)
        for zh_a in (0, 1):
            for zh_b in (0, 1):
                to = zh_b * 4 + zh_a * 2 + xh

                @pl.when(to != z)
                def _():
                    r_copy(to, xh).start()

    same = y // 2 == x % 2
    pass_half(0)
    with jax.named_scope('prod_own'):
        product(x, xg)
    pass_half(1)
    settle(x)
    for way in (0, 1):
        with jax.named_scope(f'w_x{way}'):
            for b in (0, 1):
                for j in ((2, 3), (0, 1))[way]:
                    for h in (0, 1):
                        x_copy(way, b, j, h).wait_recv()
        with jax.named_scope(f'prod_x{way}'):
            product((x_prev, x_next)[way], (x1, x2)[way])
    settle(x_prev)
    settle(x_next)

    with jax.named_scope('gather_y1'):
        @pl.when(same)
        def _():
            gather_y(x // 2)

        @pl.when(jnp.logical_not(same))
        def _():
            gather_y(0)
            gather_y(1)

    with jax.named_scope('w_far'):
        for b in (0, 1):
            for j in ORDER:
                for h in (0, 1):
                    pass_on(b, j, h).wait_recv()
    with jax.named_scope('prod_far'):
        product(x_far, x3)
    settle(x_far)

    with jax.named_scope('gather_y2'):
        @pl.when(same)
        def _():
            gather_y(1 - x // 2)

    total = s2[zl % 2, zl // 2, zh].astype(F32)
    for d in (1, 7, 2, 6, 3, 5, 4):
        with jax.named_scope(f'wr{d}'):
            r_copy((z + d) % 8, 0).wait_recv()
        total = total + rz[d - 1].astype(F32)
    mv[...] = total * (1.0 / 65536.0)
    store_m = pltpu.make_async_copy(mv, out_m, lsem.at[7])
    store_m.start()

    with jax.named_scope('tail'):
        for degree in (0, 1):
            for row in (0, 1):
                for b in (0, 1):
                    halo_copy(degree, row, b).wait_send()
        for b in (0, 1):
            for j in range(NCH):
                for h in (0, 1):
                    z_copy(h, b, j, zh).wait_send()
                    x_copy(0, b, j, h).wait_send()
                    x_copy(1, b, j, h).wait_send()
                    pass_on(b, j, h).wait_send()
        for x_a in range(4):
            for zh_a in (0, 1):
                c_copy(x_a, zh_a).wait_send()
        for d in (1, 2, 3):
            for xh in (0, 1):
                y_copy((y + d) % 4, d, xh).wait_send()
        for d in range(1, 8):
            r_copy((z + d) % 8, 0).wait_send()
        store_f.wait()
        store_m.wait()


def on_device(y_current, y_previous, h_blocks, basis_sizes, neighbours):
    tbl = make_tables(neighbours, basis_sizes)
    any_space = pl.BlockSpec(memory_space=pl.ANY)
    dma = pltpu.SemaphoreType.DMA
    halves = pltpu.VMEM((2, EL, BMAX, HB), BF)
    met = pltpu.VMEM((2, 2, GY, BMAX, HB), BF)
    return pl.pallas_call(
        main_kernel,
        out_shape=(
            jax.ShapeDtypeStruct((EL, BMAX, BD), BF),
            jax.ShapeDtypeStruct((64, BD), F32),
        ),
        in_specs=[any_space] * 4,
        out_specs=(any_space, any_space),
        scratch_shapes=[
            pltpu.SMEM((EL, 8), jnp.int32),
            halves,
            halves,
            pltpu.VMEM((EL, BMAX, 5 * BMAX), BF),
            halves,
            halves,
            *[pltpu.VMEM((GY, BMAX, HB), BF)] * 8,
            pltpu.VMEM((2, EL, BMAX, HB), F32),
            halves,
            pltpu.VMEM((EL, BMAX, BD), BF),
            met,
            met,
            met,
            met,
            pltpu.VMEM((2, 2, 2, 4, 2, 64, BD), BF),
            pltpu.VMEM((2, 2, 4, 2, 64, BD), BF),
            pltpu.VMEM((2, 2, 4, 2, 64, BD), BF),
            pltpu.VMEM((3, 2, 2, 2, 64, BD), BF),
            pltpu.VMEM((2, 2, 2, 64, BD), BF),
            pltpu.VMEM((7, 64, BD), BF),
            pltpu.VMEM((64, BD), F32),
            dma((8,)),
            dma((2, 2, 2)), dma((2, 2, 2)),
            dma((2, 2, NCH)), dma((2, 2, NCH)),
            dma((2, 2, NCH, 2)), dma((2, 2, NCH, 2)),
            dma((2, NCH, 2)), dma((2, NCH, 2)),
            dma((4, 2)), dma((4, 2)),
            dma((3, 2)), dma((3, 2)),
            dma((7,)), dma((7,)),
        ],
        compiler_params=pltpu.CompilerParams(collective_id=0, has_side_effects=True),
        name="chain",
    )(tbl, y_current, y_previous, h_blocks)


def solution(mesh):
    split = Mesh(mesh.devices.reshape(4, 4, 2, 2, 4), ELEM + BAND)
    return jax.shard_map(
        on_device,
        mesh=split,
        in_specs=(
            P(ELEM, None, BAND),
            P(ELEM, None, BAND),
            P(ELEM, None, None),
            P(ELEM),
            P(ELEM, None),
        ),
        out_specs=(P(ELEM, None, BAND), P(ELEM, BAND)),
        check_vma=False,
    )
```

time: 96.9 us -> 97.8 us (level)
  the two profiles are of different devices: /device:TPU:57 before, /device:TPU:40 now
where the time goes in v3:
time: 97.8 us; the launch traced here: 96.2 us
  Pallas kernels  92.6 us (95%)
  local copies, waits for them, and re-layouts  2.97 us (3%)
    pallas_call x1, Pallas kernels, on_device(): pl.pallas_call(main_kernel, out_shape=(jax.ShapeDtypeStruct((EL, BMAX, BD...  90.6 us
    unnamed x4, local copies, waits for them, and re-layouts  2.97 us
    pallas_call x1, Pallas kernels, make_tables(): pl.pallas_call(tables_kernel, out_shape=jax.ShapeDtypeStruct((EL, 8), jnp...  2.07 us

profile of v3, /device:TPU:40, one launch (start us, length us, event | category | flops | bytes accessed | tf_op | source)
XLA Modules:
  0.0 96.2 jit_solution(12474053558265165765)
XLA Ops:
  0.6 2.1 %tables.1.tbl_h = s32[32,8]{1,0:T(8,128)} custom-call(s32[4,32]{1,0:T(4,128)} %bitcast.1, s32[32]{0:T(128)} %sizes.1), custom_call_target="tpu_custom_call" | custom-call | tf_op jit(solution)/shard_map/tables/pallas_call | solution.py:60
  2.7 90.6 %chain.1 = (bf16[32,64,256]{2,1,0:T(8,128)(2,1)}, f32[64,256]{1,0:T(8,128)}) custom-call(s32[32,8]{1,0:T(8,128)} %tables.1.tbl_h, bf16[32,64,256]{2,1,0:T(8,128)(2,1)} %yc_h.1, bf16[32,64,256]{2,1,0:T(8,128)(2,1)} %yp_h.1, bf16[32,64,320]{2,1,0:T(8,128)(2,1)} %h_h.1), custom_call_target="tpu_custom_call" | custom-call | tf_op jit(solution)/shard_map/chain/pallas_call | solution.py:406
  93.3 0.0 copy-start
  93.3 2.3 %copy.9 = bf16[32,64,256]{2,1,0:T(8,128)(2,1)} copy(bf16[32,64,256]{2,1,0:T(8,128)(2,1)} %get-tuple-element.4) | data formatting | bytes 2097152
  95.6 0.0 copy-done
  95.6 0.6 copy.10
Async XLA Ops:
  93.3 2.3 %copy-start = (f32[64,256]{1,0:T(8,128)S(1)}, f32[64,256]{1,0:T(8,128)}, u32[]{:S(2)}) copy-start(f32[64,256]{1,0:T(8,128)} %get-tuple-element.5) | copy-start | bytes 196612

commit v4 on v3

--- a/solution.py
+++ b/solution.py
@@ -75,12 +75,14 @@
     tbl_h, yc_h, yp_h, h_h, out_f, out_m, tbl,
     yc, yp, hv, cur0, cur1, f000, f001, f010, f011, f100, f101, f110, f111,
     acc, fil, outv, xg, x1, x2, x3, pb, rc, s1, ry, s2, rz, mv,
-    lsem, hsend, hrecv, zsend, zrecv, xsend, xrecv, gsend, grecv, csend, crecv, ysend, yrecv, rsend, rrecv,
+    lsem, hsend, hrecv, zsend, zrecv, xsend, xrecv, gsend, grecv, csend, crecv, ysend, yrecv, rsend, rrecv, gate,
 ):
     zl, y, c = (lax.axis_index(a) for a in ELEM)
     zh, x = (lax.axis_index(a) for a in BAND)
     z = zh * 4 + zl
     e = (zl * 4 + y) * 2 + c
+    outer = jnp.logical_or(y == 0, y == 3)
+    crossing = jnp.logical_or(jnp.logical_and(y == 0, c == 0), jnp.logical_and(y == 3, c == 1))
 
     def elem_id(other):
         return {"zl": other // 8, "y": (other // 2) % 4, "c": other % 2}
@@ -197,8 +199,14 @@
                 for m in range(CH):
                     p = row * GY + j * CH + m
                     fil[b, p] = full_value(1, row, b, p)
-            for row in (1, 0):
-                z_copy(row, b, j, zh).start()
+            if b == 0:
+                @pl.when(jnp.logical_not(outer))
+                def _():
+                    for row in (1, 0):
+                        z_copy(row, b, j, zh).start()
+            else:
+                for row in (1, 0):
+                    z_copy(row, b, j, zh).start()
             return 0
 
         lax.fori_loop(0, NCH, one, 0)
@@ -223,6 +231,21 @@
         with jax.named_scope(f'w_h1{b}'):
             halo_copy(1, 1, b).wait_recv()
             halo_copy(1, 0, b).wait_recv()
+        if b == 1:
+            @pl.when(crossing)
+            def _():
+                pl.semaphore_signal(gate, inc=1, device_id={"c": 1 - c}, device_id_type=MESH_ID)
+
+            @pl.when(jnp.logical_and(outer, jnp.logical_not(crossing)))
+            def _():
+                with jax.named_scope('w_gate'):
+                    pl.semaphore_wait(gate, 1)
+
+            @pl.when(outer)
+            def _():
+                for j in ORDER:
+                    for row in (1, 0):
+                        z_copy(row, 0, j, zh).start()
         with jax.named_scope(f'second{b}'):
             second(b)
 
@@ -264,42 +287,39 @@
                     x_copy(j // 2, b, j, h).wait_recv()
                 pass_on(b, j, h).start()
 
-    def c_copy(x_a, zh_a):
-        at = (zh_a, x_a // 2, pl.ds((x_a % 2) * 2, 2))
-        return remote(pb.at[(1 - c, *at)], rc.at[at], csend.at[x_a, zh_a], crecv.at[x_a, zh_a], {"c": 1 - c})
-
-    def whole(ref, h):
-        return jnp.concatenate([ref[b, h].reshape(GY * BMAX, HB) for b in (0, 1)], axis=1)
-
-    def product(x_a, ref):
+    def bound_for(x_a, b):
+        return (x_a % 2) * 2 + b
+
+    def c_copy(x_a, b):
+        at = (pl.ds(0, 2), x_a // 2, bound_for(x_a, b))
+        return remote(pb.at[(1 - c, *at)], rc.at[at], csend.at[x_a, b], crecv.at[x_a, b], {"c": 1 - c})
+
+    def product(x_a, b, ref):
+        left = jnp.concatenate([ref[b, h].reshape(GY * BMAX, HB) for h in (0, 1)], axis=1)
+        for zh_b in (0, 1):
+            right = jnp.concatenate([xg[k, zh_b].reshape(GY * BMAX, HB) for k in (0, 1)], axis=1)
+            tile = lax.dot_general(left, right, (((0,), (0,)), ((), ())), preferred_element_type=F32).astype(BF)
+            for zh_a in (0, 1):
+                for core in (0, 1):
+                    at = zh_a * HB + core * 64
+                    pb[core, zh_a, x_a // 2, bound_for(x_a, b), zh_b] = tile[at : at + 64]
+        c_copy(x_a, b).start()
+
+    def y_copy(to, d, xh):
+        return remote(
+            s1.at[:, xh, to], ry.at[d - 1, xh], ysend.at[d - 1, xh], yrecv.at[d - 1, xh], {"y": to}
+        )
+
+    def settle(x_a, b):
+        xh, to = x_a // 2, bound_for(x_a, b)
+        with jax.named_scope(f'wc{b}'):
+            c_copy(x_a, b).wait_recv()
         for zh_a in (0, 1):
-            for zh_b in (0, 1):
-                tile = lax.dot_general(
-                    whole(ref, zh_a), whole(xg, zh_b), (((0,), (0,)), ((), ())), preferred_element_type=F32
-                ).astype(BF)
-                for s in range(4):
-                    pb[s % 2, zh_a, x_a // 2, (x_a % 2) * 2 + s // 2, zh_b] = tile[s * 64 : s * 64 + 64]
-            c_copy(x_a, zh_a).start()
-
-    def y_copy(to, d, xh):
-        return remote(
-            s1.at[:, xh, to], ry.at[d - 1, xh], ysend.at[d - 1, xh], yrecv.at[d - 1, xh], {"y": to}
-        )
-
-    def settle(x_a):
-        xh, pair = x_a // 2, pl.ds((x_a % 2) * 2, 2)
-        for zh_a in (0, 1):
-            with jax.named_scope(f'wc{zh_a}'):
-                c_copy(x_a, zh_a).wait_recv()
-            s1[zh_a, xh, pair] = (
-                pb[c, zh_a, xh, pair].astype(F32) + rc[zh_a, xh, pair].astype(F32)
-            ).astype(BF)
-        for k in (0, 1):
-            to = (x_a % 2) * 2 + k
-
-            @pl.when(to != y)
-            def _():
-                y_copy(to, (to + 4 - y) % 4, xh).start()
+            s1[zh_a, xh, to] = (pb[c, zh_a, xh, to].astype(F32) + rc[zh_a, xh, to].astype(F32)).astype(BF)
+
+        @pl.when(to != y)
+        def _():
+            y_copy(to, (to + 4 - y) % 4, xh).start()
 
     def r_copy(to, src_xh):
         d = (to + 8 - z) % 8
@@ -323,22 +343,40 @@
                 def _():
                     r_copy(to, xh).start()
 
-    same = y // 2 == x % 2
-    pass_half(0)
-    with jax.named_scope('prod_own'):
-        product(x, xg)
-    pass_half(1)
-    settle(x)
-    for way in (0, 1):
-        with jax.named_scope(f'w_x{way}'):
-            for b in (0, 1):
+    def beside(b):
+        for way in (0, 1):
+            with jax.named_scope(f'w_x{way}'):
                 for j in ((2, 3), (0, 1))[way]:
                     for h in (0, 1):
                         x_copy(way, b, j, h).wait_recv()
-        with jax.named_scope(f'prod_x{way}'):
-            product((x_prev, x_next)[way], (x1, x2)[way])
-    settle(x_prev)
-    settle(x_next)
+            product((x_prev, x_next)[way], b, (x1, x2)[way])
+
+    def far_unit(b):
+        with jax.named_scope(f'w_far{b}'):
+            for j in ORDER:
+                for h in (0, 1):
+                    pass_on(b, j, h).wait_recv()
+        product(x_far, b, x3)
+        settle(x_far, b)
+
+    same = y // 2 == x % 2
+    pass_half(0)
+    with jax.named_scope('prod_e'):
+        product(x, 0, xg)
+        product(x, 1, xg)
+        beside(0)
+    with jax.named_scope('settle_e'):
+        settle(x, 0)
+        settle(x, 1)
+        settle(x_prev, 0)
+        settle(x_next, 0)
+    pass_half(1)
+    with jax.named_scope('prod_l'):
+        beside(1)
+    with jax.named_scope('settle_l'):
+        settle(x_prev, 1)
+        settle(x_next, 1)
+    far_unit(0)
 
     with jax.named_scope('gather_y1'):
         @pl.when(same)
@@ -350,14 +388,7 @@
             gather_y(0)
             gather_y(1)
 
-    with jax.named_scope('w_far'):
-        for b in (0, 1):
-            for j in ORDER:
-                for h in (0, 1):
-                    pass_on(b, j, h).wait_recv()
-    with jax.named_scope('prod_far'):
-        product(x_far, x3)
-    settle(x_far)
+    far_unit(1)
 
     with jax.named_scope('gather_y2'):
         @pl.when(same)
@@ -386,8 +417,8 @@
                     x_copy(1, b, j, h).wait_send()
                     pass_on(b, j, h).wait_send()
         for x_a in range(4):
-            for zh_a in (0, 1):
-                c_copy(x_a, zh_a).wait_send()
+            for b in (0, 1):
+                c_copy(x_a, b).wait_send()
         for d in (1, 2, 3):
             for xh in (0, 1):
                 y_copy((y + d) % 4, d, xh).wait_send()
@@ -441,6 +472,7 @@
             dma((4, 2)), dma((4, 2)),
             dma((3, 2)), dma((3, 2)),
             dma((7,)), dma((7,)),
+            pltpu.SemaphoreType.REGULAR,
         ],
         compiler_params=pltpu.CompilerParams(collective_id=0, has_side_effects=True),
         name="chain",

time: 97.8 us -> 95.9 us (0.981); the launches traced: 96.2 us -> 95.7 us
  no operation moved by 1% of the time
where the time goes in v4:
time: 95.9 us; the launch traced here: 95.7 us
  Pallas kernels  92.1 us (96%)
  local copies, waits for them, and re-layouts  2.97 us (3%)
    pallas_call x1, Pallas kernels, on_device(): pl.pallas_call(main_kernel, out_shape=(jax.ShapeDtypeStruct((EL, BMAX, BD...  90 us
    unnamed x4, local copies, waits for them, and re-layouts  2.97 us
    pallas_call x1, Pallas kernels, make_tables(): pl.pallas_call(tables_kernel, out_shape=jax.ShapeDtypeStruct((EL, 8), jnp...  2.07 us

profile of v4, /device:TPU:40, one launch (start us, length us, event | category | flops | bytes accessed | tf_op | source)
XLA Modules:
  0.0 95.7 jit_solution(616210629003498934)
XLA Ops:
  0.6 2.1 %tables.1.tbl_h = s32[32,8]{1,0:T(8,128)} custom-call(s32[4,32]{1,0:T(4,128)} %bitcast.1, s32[32]{0:T(128)} %sizes.1), custom_call_target="tpu_custom_call" | custom-call | tf_op jit(solution)/shard_map/tables/pallas_call | solution.py:60
  2.7 90.0 %chain.1 = (bf16[32,64,256]{2,1,0:T(8,128)(2,1)}, f32[64,256]{1,0:T(8,128)}) custom-call(s32[32,8]{1,0:T(8,128)} %tables.1.tbl_h, bf16[32,64,256]{2,1,0:T(8,128)(2,1)} %yc_h.1, bf16[32,64,256]{2,1,0:T(8,128)(2,1)} %yp_h.1, bf16[32,64,320]{2,1,0:T(8,128)(2,1)} %h_h.1), custom_call_target="tpu_custom_call" | custom-call | tf_op jit(solution)/shard_map/chain/pallas_call | solution.py:437
  92.7 0.0 copy-start
  92.8 2.3 %copy.9 = bf16[32,64,256]{2,1,0:T(8,128)(2,1)} copy(bf16[32,64,256]{2,1,0:T(8,128)(2,1)} %get-tuple-element.4) | data formatting | bytes 2097152
  95.1 0.0 copy-done
  95.1 0.6 copy.10
Async XLA Ops:
  92.7 2.3 %copy-start = (f32[64,256]{1,0:T(8,128)S(1)}, f32[64,256]{1,0:T(8,128)}, u32[]{:S(2)}) copy-start(f32[64,256]{1,0:T(8,128)} %get-tuple-element.5) | copy-start | bytes 196612

commit v5 on v4

--- a/solution.py
+++ b/solution.py
@@ -27,62 +27,52 @@
 MESH_ID = pl.DeviceIdType.MESH
 
 
-def tables_kernel(nb, sizes, tbl, slot, mark, rank):
-    me = (lax.axis_index("zl") * 4 + lax.axis_index("y")) * 2 + lax.axis_index("c")
-    for i in range(2 * EL):
-        mark[i] = 0
-    ones = jnp.int32(0)
-    rows = []
+def ones_of(word):
+    word = word - (lax.shift_right_logical(word, 1) & 0x55555555)
+    word = (word & 0x33333333) + (lax.shift_right_logical(word, 2) & 0x33333333)
+    word = (word + lax.shift_right_logical(word, 4)) & 0x0F0F0F0F
+    return lax.shift_right_logical(word * 0x01010101, 24)
+
+
+def make_tables(me, nb, sizes, tbl, slot, link, power):
+    for i in range(EL):
+        power[i] = jnp.int32(1 << i if i < 31 else -(1 << 31))
+    ones, rows = jnp.int32(0), []
+    wanted = [jnp.int32(0), jnp.int32(0)]
     for i in range(EL):
         row = jnp.where(nb[0, i] >> 5 == me, 1, 0)
-        at = jnp.where(row == 1, GY + ones, i - ones)
-        slot[i] = at
-        tbl[at, 0] = i
-        tbl[at, 1] = sizes[i]
-        tbl[i, 6] = at
-        mark[row * EL + (nb[row, i] & (EL - 1))] = 1
+        rows.append(row)
+        slot[i] = jnp.where(row == 1, GY + ones, i - ones) & (EL - 1)
         ones = ones + row
-        rows.append(row)
-    seen = jnp.int32(0)
-    for i in range(2 * EL):
-        rank[i] = seen
-        seen = seen + mark[i]
-    for i in range(EL):
-        at, row = slot[i], rows[i]
-        tbl[at, 2] = slot[nb[1 - row, i] & (EL - 1)]
-        tbl[at, 3] = slot[nb[2, i] & (EL - 1)]
-        tbl[at, 4] = slot[nb[3, i] & (EL - 1)]
-        tbl[at, 5] = rank[row * EL + (nb[row, i] & (EL - 1))] - row * GY
-
-
-def make_tables(neighbours, basis_sizes):
-    smem = pl.BlockSpec(memory_space=pltpu.SMEM)
-    return pl.pallas_call(
-        tables_kernel,
-        out_shape=jax.ShapeDtypeStruct((EL, 8), jnp.int32),
-        in_specs=[smem, smem],
-        out_specs=smem,
-        scratch_shapes=[
-            pltpu.SMEM((EL,), jnp.int32),
-            pltpu.SMEM((2 * EL,), jnp.int32),
-            pltpu.SMEM((2 * EL,), jnp.int32),
-        ],
-        name="tables",
-    )(neighbours.T, basis_sizes)
+        for k in (0, 1):
+            wanted[k] = wanted[k] + jnp.where(row == k, power[nb[k, i] & (EL - 1)], 0)
+    first = [jnp.int32(0), jnp.int32(0)]
+    for i in reversed(range(EL)):
+        link[i] = jnp.where(rows[i] == 1, first[1], first[0])
+        first = [jnp.where(rows[i] == k, i, first[k]) for k in (0, 1)]
+    for row in (0, 1):
+        i = first[row]
+        for p in range(row * GY, row * GY + GY):
+            tbl[p, 0] = i
+            tbl[p, 1] = sizes[i]
+            tbl[p, 2] = slot[nb[1 - row, i] & (EL - 1)]
+            tbl[p, 3] = slot[nb[2, i] & (EL - 1)]
+            tbl[p, 4] = slot[nb[3, i] & (EL - 1)]
+            tbl[p, 5] = ones_of(wanted[row] & (power[nb[row, i] & (EL - 1)] - 1)) & (GY - 1)
+            i = link[i]
 
 
 def main_kernel(
-    tbl_h, yc_h, yp_h, h_h, out_f, out_m, tbl,
+    nb_h, size_h, yc_h, yp_h, h_h, out_f, out_m, nb, sizes, tbl, slot, link, power,
     yc, yp, hv, cur0, cur1, f000, f001, f010, f011, f100, f101, f110, f111,
     acc, fil, outv, xg, x1, x2, x3, pb, rc, s1, ry, s2, rz, mv,
-    lsem, hsend, hrecv, zsend, zrecv, xsend, xrecv, gsend, grecv, csend, crecv, ysend, yrecv, rsend, rrecv, gate,
+    lsem, hsend, hrecv, zsend, zrecv, xsend, xrecv, gsend, grecv, csend, crecv, ysend, yrecv, rsend, rrecv,
 ):
     zl, y, c = (lax.axis_index(a) for a in ELEM)
     zh, x = (lax.axis_index(a) for a in BAND)
     z = zh * 4 + zl
     e = (zl * 4 + y) * 2 + c
     outer = jnp.logical_or(y == 0, y == 3)
-    crossing = jnp.logical_or(jnp.logical_and(y == 0, c == 0), jnp.logical_and(y == 3, c == 1))
 
     def elem_id(other):
         return {"zl": other // 8, "y": (other // 2) % 4, "c": other % 2}
@@ -102,7 +92,7 @@
     loads = [
         pltpu.make_async_copy(src, dst, lsem.at[k])
         for k, (src, dst) in enumerate(
-            [(tbl_h, tbl)]
+            [(nb_h, nb), (size_h, sizes)]
             + [(yc_h.at[:, :, pl.ds(b * HB, HB)], yc.at[b]) for b in (0, 1)]
             + [(h_h, hv)]
             + [(yp_h.at[:, :, pl.ds(b * HB, HB)], yp.at[b]) for b in (0, 1)]
@@ -122,8 +112,12 @@
     zero = jnp.zeros((BMAX, HB), BF)
 
     with jax.named_scope('w_load'):
-        for load in loads[:3]:
+        for load in loads[:2]:
             load.wait()
+    with jax.named_scope('tables'):
+        make_tables(e, nb, sizes, tbl, slot, link, power)
+    for load in loads[2:4]:
+        load.wait()
 
     def pack(row, b):
         def one(p, _):
@@ -152,7 +146,7 @@
     halo_copy(0, 0, 1).start()
     pack(0, 1)
     halo_copy(0, 1, 1).start()
-    for load in loads[3:]:
+    for load in loads[4:]:
         load.wait()
 
     def local_part(degree, row, b):
@@ -186,11 +180,31 @@
 
         lax.fori_loop(row * GY, row * GY + GY, one, 0, unroll=8)
 
-    def z_copy(half, b, j, src_zh):
+    def z_copy(half, b, j):
         return remote(
-            fil.at[b, pl.ds(half * GY + j * CH, CH)], xg.at[b, src_zh, pl.ds(j * CH, CH)],
-            zsend.at[half, b, j], zrecv.at[src_zh, b, j], z_id((zl + 2 + 4 * half) % 8),
-        )
+            fil.at[b, pl.ds(half * GY + j * CH, CH)], xg.at[b, zh, pl.ds(j * CH, CH)],
+            zsend.at[half, b], zrecv.at[b, j], z_id((zl + 2 + 4 * half) % 8),
+        )
+
+    def x_copy(way, b, j):
+        part = pl.ds(j * CH, CH)
+        return remote(
+            xg.at[b, :, part], (x1, x2)[way].at[b, :, part], xsend.at[way, b], xrecv.at[way, b, j], (xp, xm)[way]
+        )
+
+    def pass_on(b, j):
+        part, way = pl.ds(j * CH, CH), j // 2
+        return remote((x1, x2)[way].at[b, :, part], x3.at[b, :, part], gsend.at[b], grecv.at[b, j], (xp, xm)[way])
+
+    def bytes_of(ref, sem):
+        return pltpu.make_async_copy(ref, ref, sem)
+
+    def z_to_x(b):
+        for j in ORDER:
+            with jax.named_scope(f'wz{b}{j}'):
+                bytes_of(xg.at[b, :, pl.ds(j * CH, CH)], zrecv.at[b, j]).wait()
+            x_copy(0, b, j).start()
+            x_copy(1, b, j).start()
 
     def second(b):
         def one(k, _):
@@ -199,14 +213,8 @@
                 for m in range(CH):
                     p = row * GY + j * CH + m
                     fil[b, p] = full_value(1, row, b, p)
-            if b == 0:
-                @pl.when(jnp.logical_not(outer))
-                def _():
-                    for row in (1, 0):
-                        z_copy(row, b, j, zh).start()
-            else:
-                for row in (1, 0):
-                    z_copy(row, b, j, zh).start()
+            for row in (1, 0):
+                z_copy(row, b, j).start()
             return 0
 
         lax.fori_loop(0, NCH, one, 0)
@@ -227,72 +235,49 @@
         with jax.named_scope(f'local1{b}'):
             local_part(1, 1, b)
             local_part(1, 0, b)
-    for b in (0, 1):
+    def finish(b):
         with jax.named_scope(f'w_h1{b}'):
             halo_copy(1, 1, b).wait_recv()
             halo_copy(1, 0, b).wait_recv()
-        if b == 1:
-            @pl.when(crossing)
-            def _():
-                pl.semaphore_signal(gate, inc=1, device_id={"c": 1 - c}, device_id_type=MESH_ID)
-
-            @pl.when(jnp.logical_and(outer, jnp.logical_not(crossing)))
-            def _():
-                with jax.named_scope('w_gate'):
-                    pl.semaphore_wait(gate, 1)
-
-            @pl.when(outer)
-            def _():
-                for j in ORDER:
-                    for row in (1, 0):
-                        z_copy(row, 0, j, zh).start()
         with jax.named_scope(f'second{b}'):
             second(b)
 
+    finish(0)
+
+    @pl.when(outer)
+    def _():
+        z_to_x(0)
+
+    finish(1)
+
+    @pl.when(jnp.logical_not(outer))
+    def _():
+        z_to_x(0)
+
+    z_to_x(1)
+
     def put(i, _):
-        s = tbl[i, 6]
+        s = slot[i]
         outv[i] = jnp.concatenate([fil[0, s], fil[1, s]], axis=1)
         return 0
 
     with jax.named_scope('put'):
         lax.fori_loop(0, EL, put, 0, unroll=4)
-    store_f = pltpu.make_async_copy(outv, out_f, lsem.at[6])
+    store_f = pltpu.make_async_copy(outv, out_f, lsem.at[7])
     store_f.start()
-
-    def x_copy(way, b, j, h):
-        part = pl.ds(j * CH, CH)
-        return remote(
-            xg.at[b, h, part], (x1, x2)[way].at[b, h, part],
-            xsend.at[way, b, j, h], xrecv.at[way, b, j, h], (xp, xm)[way],
-        )
-
-    def pass_on(b, j, h):
-        part, way = pl.ds(j * CH, CH), j // 2
-        return remote(
-            (x1, x2)[way].at[b, h, part], x3.at[b, h, part], gsend.at[b, j, h], grecv.at[b, j, h], (xp, xm)[way]
-        )
-
-    for b in (0, 1):
-        for j in ORDER:
-            for h in (0, 1):
-                with jax.named_scope(f'wz{b}{j}{h}'):
-                    z_copy(0, b, j, h).wait_recv()
-                x_copy(0, b, j, h).start()
-                x_copy(1, b, j, h).start()
 
     def pass_half(b):
         for j in ORDER:
-            for h in (0, 1):
-                with jax.named_scope(f'wx{b}{j}{h}'):
-                    x_copy(j // 2, b, j, h).wait_recv()
-                pass_on(b, j, h).start()
+            with jax.named_scope(f'wx{b}{j}'):
+                x_copy(j // 2, b, j).wait_recv()
+            pass_on(b, j).start()
 
     def bound_for(x_a, b):
         return (x_a % 2) * 2 + b
 
     def c_copy(x_a, b):
         at = (pl.ds(0, 2), x_a // 2, bound_for(x_a, b))
-        return remote(pb.at[(1 - c, *at)], rc.at[at], csend.at[x_a, b], crecv.at[x_a, b], {"c": 1 - c})
+        return remote(pb.at[(1 - c, *at)], rc.at[at], csend, crecv.at[x_a, b], {"c": 1 - c})
 
     def product(x_a, b, ref):
         left = jnp.concatenate([ref[b, h].reshape(GY * BMAX, HB) for h in (0, 1)], axis=1)
@@ -307,7 +292,7 @@
 
     def y_copy(to, d, xh):
         return remote(
-            s1.at[:, xh, to], ry.at[d - 1, xh], ysend.at[d - 1, xh], yrecv.at[d - 1, xh], {"y": to}
+            s1.at[:, xh, to], ry.at[d - 1, xh], ysend, yrecv.at[d - 1, xh], {"y": to}
         )
 
     def settle(x_a, b):
@@ -324,7 +309,7 @@
     def r_copy(to, src_xh):
         d = (to + 8 - z) % 8
         return remote(
-            s2.at[src_xh, (to % 4) // 2, to // 4], rz.at[d - 1], rsend.at[d - 1], rrecv.at[d - 1], z_id(to)
+            s2.at[src_xh, (to % 4) // 2, to // 4], rz.at[d - 1], rsend, rrecv, z_id(to)
         )
 
     def gather_y(xh):
@@ -347,15 +332,13 @@
         for way in (0, 1):
             with jax.named_scope(f'w_x{way}'):
                 for j in ((2, 3), (0, 1))[way]:
-                    for h in (0, 1):
-                        x_copy(way, b, j, h).wait_recv()
+                    x_copy(way, b, j).wait_recv()
             product((x_prev, x_next)[way], b, (x1, x2)[way])
 
     def far_unit(b):
         with jax.named_scope(f'w_far{b}'):
             for j in ORDER:
-                for h in (0, 1):
-                    pass_on(b, j, h).wait_recv()
+                pass_on(b, j).wait_recv()
         product(x_far, b, x3)
         settle(x_far, b)
 
@@ -377,6 +360,7 @@
         settle(x_prev, 1)
         settle(x_next, 1)
     far_unit(0)
+    far_unit(1)
 
     with jax.named_scope('gather_y1'):
         @pl.when(same)
@@ -388,20 +372,18 @@
             gather_y(0)
             gather_y(1)
 
-    far_unit(1)
-
     with jax.named_scope('gather_y2'):
         @pl.when(same)
         def _():
             gather_y(1 - x // 2)
 
     total = s2[zl % 2, zl // 2, zh].astype(F32)
-    for d in (1, 7, 2, 6, 3, 5, 4):
-        with jax.named_scope(f'wr{d}'):
-            r_copy((z + d) % 8, 0).wait_recv()
-        total = total + rz[d - 1].astype(F32)
+    with jax.named_scope('wr'):
+        bytes_of(rz, rrecv).wait()
+    for d in range(7):
+        total = total + rz[d].astype(F32)
     mv[...] = total * (1.0 / 65536.0)
-    store_m = pltpu.make_async_copy(mv, out_m, lsem.at[7])
+    store_m = pltpu.make_async_copy(mv, out_m, lsem.at[8])
     store_m.start()
 
     with jax.named_scope('tail'):
@@ -410,26 +392,18 @@
                 for b in (0, 1):
                     halo_copy(degree, row, b).wait_send()
         for b in (0, 1):
-            for j in range(NCH):
-                for h in (0, 1):
-                    z_copy(h, b, j, zh).wait_send()
-                    x_copy(0, b, j, h).wait_send()
-                    x_copy(1, b, j, h).wait_send()
-                    pass_on(b, j, h).wait_send()
-        for x_a in range(4):
-            for b in (0, 1):
-                c_copy(x_a, b).wait_send()
-        for d in (1, 2, 3):
-            for xh in (0, 1):
-                y_copy((y + d) % 4, d, xh).wait_send()
-        for d in range(1, 8):
-            r_copy((z + d) % 8, 0).wait_send()
+            for k in (0, 1):
+                bytes_of(fil.at[b, pl.ds(k * GY, GY)], zsend.at[k, b]).wait()
+                bytes_of(xg.at[b], xsend.at[k, b]).wait()
+            bytes_of(x3.at[b], gsend.at[b]).wait()
+        bytes_of(rc, csend).wait()
+        bytes_of(ry, ysend).wait()
+        bytes_of(rz, rsend).wait()
         store_f.wait()
         store_m.wait()
 
 
 def on_device(y_current, y_previous, h_blocks, basis_sizes, neighbours):
-    tbl = make_tables(neighbours, basis_sizes)
     any_space = pl.BlockSpec(memory_space=pl.ANY)
     dma = pltpu.SemaphoreType.DMA
     halves = pltpu.VMEM((2, EL, BMAX, HB), BF)
@@ -440,10 +414,15 @@
             jax.ShapeDtypeStruct((EL, BMAX, BD), BF),
             jax.ShapeDtypeStruct((64, BD), F32),
         ),
-        in_specs=[any_space] * 4,
+        in_specs=[any_space] * 5,
         out_specs=(any_space, any_space),
         scratch_shapes=[
+            pltpu.SMEM((4, EL), jnp.int32),
+            pltpu.SMEM((EL,), jnp.int32),
             pltpu.SMEM((EL, 8), jnp.int32),
+            pltpu.SMEM((EL,), jnp.int32),
+            pltpu.SMEM((EL,), jnp.int32),
+            pltpu.SMEM((EL,), jnp.int32),
             halves,
             halves,
             pltpu.VMEM((EL, BMAX, 5 * BMAX), BF),
@@ -464,19 +443,18 @@
             pltpu.VMEM((2, 2, 2, 64, BD), BF),
             pltpu.VMEM((7, 64, BD), BF),
             pltpu.VMEM((64, BD), F32),
-            dma((8,)),
+            dma((9,)),
             dma((2, 2, 2)), dma((2, 2, 2)),
-            dma((2, 2, NCH)), dma((2, 2, NCH)),
-            dma((2, 2, NCH, 2)), dma((2, 2, NCH, 2)),
-            dma((2, NCH, 2)), dma((2, NCH, 2)),
-            dma((4, 2)), dma((4, 2)),
-            dma((3, 2)), dma((3, 2)),
-            dma((7,)), dma((7,)),
-            pltpu.SemaphoreType.REGULAR,
+            dma((2, 2)), dma((2, NCH)),
+            dma((2, 2)), dma((2, 2, NCH)),
+            dma((2,)), dma((2, NCH)),
+            dma, dma((4, 2)),
+            dma, dma((3, 2)),
+            dma, dma,
         ],
         compiler_params=pltpu.CompilerParams(collective_id=0, has_side_effects=True),
         name="chain",
-    )(tbl, y_current, y_previous, h_blocks)
+    )(neighbours.T, basis_sizes, y_current, y_previous, h_blocks)
 
 
 def solution(mesh):

time: 95.9 us -> 86.4 us (0.901)
  Pallas kernels: 92.1 us -> 82.4 us
    pallas_call x1, Pallas kernels: 90 us -> 82.4 us  [on_device(): pl.pallas_call(main_kernel, out_shape=(jax.ShapeDtypeStruct((EL, BMAX, BD...]
    pallas_call x1 -> x0, Pallas kernels: 2.07 us -> none  [make_tables(): pl.pallas_call(tables_kernel, out_shape=jax.ShapeDtypeStruct((EL, 8), jnp...]
where the time goes in v5:
time: 86.4 us; the launch traced here: 86 us
  Pallas kernels  82.4 us (95%)
  local copies, waits for them, and re-layouts  2.97 us (3%)
    pallas_call x1, Pallas kernels, on_device(): pl.pallas_call(main_kernel, out_shape=(jax.ShapeDtypeStruct((EL, BMAX, BD...  82.4 us
    unnamed x4, local copies, waits for them, and re-layouts  2.97 us

profile of v5, /device:TPU:40, one launch (start us, length us, event | category | flops | bytes accessed | tf_op | source)
XLA Modules:
  0.0 86.0 jit_solution(15916854715096638903)
XLA Ops:
  0.6 82.4 %chain.1 = (bf16[32,64,256]{2,1,0:T(8,128)(2,1)}, f32[64,256]{1,0:T(8,128)}) custom-call(s32[4,32]{1,0:T(4,128)} %bitcast.1, s32[32]{0:T(128)} %size_h.1, bf16[32,64,256]{2,1,0:T(8,128)(2,1)} %yc_h.1, bf16[32,64,256]{2,1,0:T(8,128)(2,1)} %yp_h.1, bf16[32,64,320]{2,1,0:T(8,128)(2,1)} %h_h.1), custom_call_target="tpu_custom_call" | custom-call | tf_op jit(solution)/shard_map/chain/pallas_call | solution.py:411
  83.1 0.0 copy-start
  83.1 2.3 %copy.9 = bf16[32,64,256]{2,1,0:T(8,128)(2,1)} copy(bf16[32,64,256]{2,1,0:T(8,128)(2,1)} %get-tuple-element.4) | data formatting | bytes 2097152
  85.4 0.0 copy-done
  85.4 0.6 copy.10
Async XLA Ops:
  83.1 2.3 %copy-start = (f32[64,256]{1,0:T(8,128)S(1)}, f32[64,256]{1,0:T(8,128)}, u32[]{:S(2)}) copy-start(f32[64,256]{1,0:T(8,128)} %get-tuple-element.5) | copy-start | bytes 196612

commit v6 on v5

--- a/solution.py
+++ b/solution.py
@@ -65,8 +65,8 @@
 def main_kernel(
     nb_h, size_h, yc_h, yp_h, h_h, out_f, out_m, nb, sizes, tbl, slot, link, power,
     yc, yp, hv, cur0, cur1, f000, f001, f010, f011, f100, f101, f110, f111,
-    acc, fil, outv, xg, x1, x2, x3, pb, rc, s1, ry, s2, rz, mv,
-    lsem, hsend, hrecv, zsend, zrecv, xsend, xrecv, gsend, grecv, csend, crecv, ysend, yrecv, rsend, rrecv,
+    acc, fil, outv, xg, x1, x2, x3, pb, rc, s1, ry, s2, rz, mv, ft, fr,
+    lsem, hsend, hrecv, zsend, zrecv, xsend, xrecv, gsend, grecv, csend, crecv, ysend, yrecv, rsend, rrecv, fsend, frecv,
 ):
     zl, y, c = (lax.axis_index(a) for a in ELEM)
     zh, x = (lax.axis_index(a) for a in BAND)
@@ -108,6 +108,18 @@
     for to in partners:
         pl.semaphore_signal(barrier, inc=1, device_id=to, device_id_type=MESH_ID)
 
+    same = y // 2 == x % 2
+    mirrored = jnp.logical_not(same)
+    b_own, b_rows = zh * 4 + x, e // 4
+
+    def mirror_id(s):
+        return {**elem_id(4 * b_own + s), "zh": b_rows // 4, "x": b_rows % 4}
+
+    @pl.when(mirrored)
+    def _():
+        for s in range(4):
+            pl.semaphore_signal(barrier, inc=1, device_id=mirror_id(s), device_id_type=MESH_ID)
+
     rows = lax.broadcasted_iota(jnp.int32, (BMAX, HB), 0)
     zero = jnp.zeros((BMAX, HB), BF)
 
@@ -138,7 +150,7 @@
     with jax.named_scope('pack'):
         pack(1, 0)
     with jax.named_scope('barrier'):
-        pl.semaphore_wait(barrier, len(partners))
+        pl.semaphore_wait(barrier, len(partners) + 4 * mirrored.astype(jnp.int32))
     halo_copy(0, 0, 0).start()
     pack(0, 0)
     halo_copy(0, 1, 0).start()
@@ -186,25 +198,30 @@
             zsend.at[half, b], zrecv.at[b, j], z_id((zl + 2 + 4 * half) % 8),
         )
 
-    def x_copy(way, b, j):
-        part = pl.ds(j * CH, CH)
+    def x_copy(b, j):
+        way, at = j // 2, pl.ds(j % 2 * CH, CH)
         return remote(
-            xg.at[b, :, part], (x1, x2)[way].at[b, :, part], xsend.at[way, b], xrecv.at[way, b, j], (xp, xm)[way]
+            xg.at[b, :, pl.ds(j * CH, CH)], (x1, x2)[way].at[b, :, at], xsend.at[b], xrecv.at[b, j], (xp, xm)[way]
         )
 
     def pass_on(b, j):
-        part, way = pl.ds(j * CH, CH), j // 2
-        return remote((x1, x2)[way].at[b, :, part], x3.at[b, :, part], gsend.at[b], grecv.at[b, j], (xp, xm)[way])
+        way, at = j // 2, pl.ds(j % 2 * CH, CH)
+        return remote(
+            (x1, x2)[way].at[b, :, at], x3.at[b, :, pl.ds(j * CH, CH)], gsend.at[b], grecv.at[b, j], (xp, xm)[way]
+        )
 
     def bytes_of(ref, sem):
         return pltpu.make_async_copy(ref, ref, sem)
 
-    def z_to_x(b):
-        for j in ORDER:
-            with jax.named_scope(f'wz{b}{j}'):
-                bytes_of(xg.at[b, :, pl.ds(j * CH, CH)], zrecv.at[b, j]).wait()
-            x_copy(0, b, j).start()
-            x_copy(1, b, j).start()
+    def z_to_x(b, j):
+        with jax.named_scope(f'wz{b}{j}'):
+            bytes_of(xg.at[b, :, pl.ds(j * CH, CH)], zrecv.at[b, j]).wait()
+        x_copy(b, j).start()
+
+    def x_to_far(b, j):
+        with jax.named_scope(f'wx{b}{j}'):
+            x_copy(b, j).wait_recv()
+        pass_on(b, j).start()
 
     def second(b):
         def one(k, _):
@@ -246,15 +263,25 @@
 
     @pl.when(outer)
     def _():
-        z_to_x(0)
+        for j in ORDER:
+            z_to_x(0, j)
 
     finish(1)
 
     @pl.when(jnp.logical_not(outer))
     def _():
-        z_to_x(0)
-
-    z_to_x(1)
+        for j in ORDER:
+            z_to_x(0, j)
+
+    for j in ORDER[:3]:
+        x_to_far(0, j)
+    z_to_x(1, ORDER[0])
+    x_to_far(0, ORDER[3])
+    z_to_x(1, ORDER[1])
+    z_to_x(1, ORDER[2])
+    x_to_far(1, ORDER[0])
+    z_to_x(1, ORDER[3])
+    x_to_far(1, ORDER[1])
 
     def put(i, _):
         s = slot[i]
@@ -266,12 +293,6 @@
     store_f = pltpu.make_async_copy(outv, out_f, lsem.at[7])
     store_f.start()
 
-    def pass_half(b):
-        for j in ORDER:
-            with jax.named_scope(f'wx{b}{j}'):
-                x_copy(j // 2, b, j).wait_recv()
-            pass_on(b, j).start()
-
     def bound_for(x_a, b):
         return (x_a % 2) * 2 + b
 
@@ -279,10 +300,12 @@
         at = (pl.ds(0, 2), x_a // 2, bound_for(x_a, b))
         return remote(pb.at[(1 - c, *at)], rc.at[at], csend, crecv.at[x_a, b], {"c": 1 - c})
 
-    def product(x_a, b, ref):
-        left = jnp.concatenate([ref[b, h].reshape(GY * BMAX, HB) for h in (0, 1)], axis=1)
+    def product(x_a, b, ref, first_row=0):
+        count = ref.shape[2]
+        part = pl.ds(first_row, count)
+        left = jnp.concatenate([ref[b, h].reshape(count * BMAX, HB) for h in (0, 1)], axis=1)
         for zh_b in (0, 1):
-            right = jnp.concatenate([xg[k, zh_b].reshape(GY * BMAX, HB) for k in (0, 1)], axis=1)
+            right = jnp.concatenate([xg[k, zh_b, part].reshape(count * BMAX, HB) for k in (0, 1)], axis=1)
             tile = lax.dot_general(left, right, (((0,), (0,)), ((), ())), preferred_element_type=F32).astype(BF)
             for zh_a in (0, 1):
                 for core in (0, 1):
@@ -329,60 +352,67 @@
                     r_copy(to, xh).start()
 
     def beside(b):
-        for way in (0, 1):
-            with jax.named_scope(f'w_x{way}'):
-                for j in ((2, 3), (0, 1))[way]:
-                    x_copy(way, b, j).wait_recv()
-            product((x_prev, x_next)[way], b, (x1, x2)[way])
+        product(x_prev, b, x1)
+        product(x_next, b, x2, GY // 2)
 
     def far_unit(b):
         with jax.named_scope(f'w_far{b}'):
             for j in ORDER:
                 pass_on(b, j).wait_recv()
         product(x_far, b, x3)
-        settle(x_far, b)
-
-    same = y // 2 == x % 2
-    pass_half(0)
+
     with jax.named_scope('prod_e'):
+        beside(0)
         product(x, 0, xg)
         product(x, 1, xg)
-        beside(0)
-    with jax.named_scope('settle_e'):
-        settle(x, 0)
-        settle(x, 1)
-        settle(x_prev, 0)
-        settle(x_next, 0)
-    pass_half(1)
+    x_to_far(1, ORDER[2])
+    x_to_far(1, ORDER[3])
     with jax.named_scope('prod_l'):
         beside(1)
-    with jax.named_scope('settle_l'):
-        settle(x_prev, 1)
-        settle(x_next, 1)
+    with jax.named_scope('settle'):
+        for x_a, b in ((x_prev, 0), (x_next, 0), (x_prev, 1), (x_next, 1), (x, 0), (x, 1)):
+            settle(x_a, b)
     far_unit(0)
     far_unit(1)
-
-    with jax.named_scope('gather_y1'):
+    with jax.named_scope('settle_far'):
+        settle(x_far, 0)
+        settle(x_far, 1)
+
+    with jax.named_scope('gather_y'):
         @pl.when(same)
         def _():
             gather_y(x // 2)
-
-        @pl.when(jnp.logical_not(same))
+            gather_y(1 - x // 2)
+
+        @pl.when(mirrored)
         def _():
             gather_y(0)
             gather_y(1)
-
-    with jax.named_scope('gather_y2'):
-        @pl.when(same)
-        def _():
-            gather_y(1 - x // 2)
 
     total = s2[zl % 2, zl // 2, zh].astype(F32)
     with jax.named_scope('wr'):
         bytes_of(rz, rrecv).wait()
     for d in range(7):
         total = total + rz[d].astype(F32)
-    mv[...] = total * (1.0 / 65536.0)
+    total = total * (1.0 / 65536.0)
+    mv[...] = total
+
+    def f_copy(s, to):
+        return remote(ft.at[s], fr.at[to], fsend.at[s], frecv.at[to], mirror_id(s))
+
+    @pl.when(mirrored)
+    def _():
+        turned = total.T.astype(BF)
+        for s in range(4):
+            ft[s] = turned[s * 64 : s * 64 + 64]
+            f_copy(s, e % 4).start()
+        with jax.named_scope('w_mirror'):
+            for s in range(4):
+                f_copy(s, s).wait_recv()
+        mv[...] = mv[...] + jnp.concatenate([fr[s].astype(F32) for s in range(4)], axis=1)
+        for s in range(4):
+            f_copy(s, e % 4).wait_send()
+
     store_m = pltpu.make_async_copy(mv, out_m, lsem.at[8])
     store_m.start()
 
@@ -394,7 +424,7 @@
         for b in (0, 1):
             for k in (0, 1):
                 bytes_of(fil.at[b, pl.ds(k * GY, GY)], zsend.at[k, b]).wait()
-                bytes_of(xg.at[b], xsend.at[k, b]).wait()
+            bytes_of(xg.at[b], xsend.at[b]).wait()
             bytes_of(x3.at[b], gsend.at[b]).wait()
         bytes_of(rc, csend).wait()
         bytes_of(ry, ysend).wait()
@@ -433,8 +463,8 @@
             halves,
             pltpu.VMEM((EL, BMAX, BD), BF),
             met,
-            met,
-            met,
+            pltpu.VMEM((2, 2, GY // 2, BMAX, HB), BF),
+            pltpu.VMEM((2, 2, GY // 2, BMAX, HB), BF),
             met,
             pltpu.VMEM((2, 2, 2, 4, 2, 64, BD), BF),
             pltpu.VMEM((2, 2, 4, 2, 64, BD), BF),
@@ -443,14 +473,17 @@
             pltpu.VMEM((2, 2, 2, 64, BD), BF),
             pltpu.VMEM((7, 64, BD), BF),
             pltpu.VMEM((64, BD), F32),
+            pltpu.VMEM((4, 64, 64), BF),
+            pltpu.VMEM((4, 64, 64), BF),
             dma((9,)),
             dma((2, 2, 2)), dma((2, 2, 2)),
             dma((2, 2)), dma((2, NCH)),
-            dma((2, 2)), dma((2, 2, NCH)),
+            dma((2,)), dma((2, NCH)),
             dma((2,)), dma((2, NCH)),
             dma, dma((4, 2)),
             dma, dma((3, 2)),
             dma, dma,
+            dma((4,)), dma((4,)),
         ],
         compiler_params=pltpu.CompilerParams(collective_id=0, has_side_effects=True),
         name="chain",

time: 86.4 us -> 87.9 us (1.017)
  the two profiles are of different devices: /device:TPU:40 before, /device:TPU:71 now
where the time goes in v6:
time: 87.9 us; the launch traced here: 87.7 us
  Pallas kernels  84.1 us (96%)
  local copies, waits for them, and re-layouts  2.97 us (3%)
    pallas_call x1, Pallas kernels, on_device(): pl.pallas_call(main_kernel, out_shape=(jax.ShapeDtypeStruct((EL, BMAX, BD...  84.1 us
    unnamed x4, local copies, waits for them, and re-layouts  2.97 us

profile of v6, /device:TPU:71, one launch (start us, length us, event | category | flops | bytes accessed | tf_op | source)
XLA Modules:
  0.0 87.7 jit_solution(14632024023152059360)
XLA Ops:
  0.6 84.1 %chain.1 = (bf16[32,64,256]{2,1,0:T(8,128)(2,1)}, f32[64,256]{1,0:T(8,128)}) custom-call(s32[4,32]{1,0:T(4,128)} %bitcast.1, s32[32]{0:T(128)} %size_h.1, bf16[32,64,256]{2,1,0:T(8,128)(2,1)} %yc_h.1, bf16[32,64,256]{2,1,0:T(8,128)(2,1)} %yp_h.1, bf16[32,64,320]{2,1,0:T(8,128)(2,1)} %h_h.1), custom_call_target="tpu_custom_call" | custom-call | tf_op jit(solution)/shard_map/chain/pallas_call | solution.py:441
  84.8 0.0 copy-start
  84.8 2.3 %copy.9 = bf16[32,64,256]{2,1,0:T(8,128)(2,1)} copy(bf16[32,64,256]{2,1,0:T(8,128)(2,1)} %get-tuple-element.4) | data formatting | bytes 2097152
  87.1 0.0 copy-done
  87.1 0.6 copy.10
Async XLA Ops:
  84.8 2.3 %copy-start = (f32[64,256]{1,0:T(8,128)S(1)}, f32[64,256]{1,0:T(8,128)}, u32[]{:S(2)}) copy-start(f32[64,256]{1,0:T(8,128)} %get-tuple-element.5) | copy-start | bytes 196612

commit v7 on v6

--- a/solution.py
+++ b/solution.py
@@ -110,15 +110,14 @@
 
     same = y // 2 == x % 2
     mirrored = jnp.logical_not(same)
-    b_own, b_rows = zh * 4 + x, e // 4
-
-    def mirror_id(s):
-        return {**elem_id(4 * b_own + s), "zh": b_rows // 4, "x": b_rows % 4}
+    b_rows = e // 4
 
     @pl.when(mirrored)
     def _():
-        for s in range(4):
-            pl.semaphore_signal(barrier, inc=1, device_id=mirror_id(s), device_id_type=MESH_ID)
+        for other in range(8):
+            for s in range(4):
+                source = {**z_id(other), "y": x % 2 * 2 + s // 2, "c": s % 2, "x": b_rows % 4}
+                pl.semaphore_signal(barrier, inc=1, device_id=source, device_id_type=MESH_ID)
 
     rows = lax.broadcasted_iota(jnp.int32, (BMAX, HB), 0)
     zero = jnp.zeros((BMAX, HB), BF)
@@ -150,7 +149,7 @@
     with jax.named_scope('pack'):
         pack(1, 0)
     with jax.named_scope('barrier'):
-        pl.semaphore_wait(barrier, len(partners) + 4 * mirrored.astype(jnp.int32))
+        pl.semaphore_wait(barrier, len(partners) + 32 * mirrored.astype(jnp.int32))
     halo_copy(0, 0, 0).start()
     pack(0, 0)
     halo_copy(0, 1, 0).start()
@@ -277,21 +276,13 @@
         x_to_far(0, j)
     z_to_x(1, ORDER[0])
     x_to_far(0, ORDER[3])
-    z_to_x(1, ORDER[1])
-    z_to_x(1, ORDER[2])
-    x_to_far(1, ORDER[0])
-    z_to_x(1, ORDER[3])
-    x_to_far(1, ORDER[1])
+    for j in ORDER[1:]:
+        z_to_x(1, j)
 
     def put(i, _):
         s = slot[i]
         outv[i] = jnp.concatenate([fil[0, s], fil[1, s]], axis=1)
         return 0
-
-    with jax.named_scope('put'):
-        lax.fori_loop(0, EL, put, 0, unroll=4)
-    store_f = pltpu.make_async_copy(outv, out_f, lsem.at[7])
-    store_f.start()
 
     def bound_for(x_a, b):
         return (x_a % 2) * 2 + b
@@ -335,6 +326,11 @@
             s2.at[src_xh, (to % 4) // 2, to // 4], rz.at[d - 1], rsend, rrecv, z_id(to)
         )
 
+    def f_copy(xh, zh_a, zh_b, s):
+        tile_rows, tile_columns = (zh_a * 2 + xh) * 2 + y // 2, zh_b * 4 + x
+        to = {**elem_id(4 * tile_columns + s), "zh": tile_rows // 4, "x": tile_rows % 4}
+        return remote(ft.at[xh, zh_a, zh_b, s], fr.at[e % 4, z], fsend, frecv, to)
+
     def gather_y(xh):
         for d in (1, 3, 2):
             y_copy((y + d) % 4, d, xh).wait_recv()
@@ -351,6 +347,15 @@
                 def _():
                     r_copy(to, xh).start()
 
+        @pl.when(mirrored)
+        def _():
+            for zh_a in (0, 1):
+                for zh_b in (0, 1):
+                    turned = s2[xh, zh_a, zh_b].astype(F32).T.astype(BF)
+                    for s in range(4):
+                        ft[xh, zh_a, zh_b, s] = turned[s * 64 : s * 64 + 64]
+                        f_copy(xh, zh_a, zh_b, s).start()
+
     def beside(b):
         product(x_prev, b, x1)
         product(x_next, b, x2, GY // 2)
@@ -365,17 +370,26 @@
         beside(0)
         product(x, 0, xg)
         product(x, 1, xg)
-    x_to_far(1, ORDER[2])
-    x_to_far(1, ORDER[3])
+    with jax.named_scope('settle_e'):
+        for x_a, b in ((x_prev, 0), (x_next, 0), (x, 0), (x, 1)):
+            settle(x_a, b)
+    for j in ORDER:
+        x_to_far(1, j)
+    with jax.named_scope('put'):
+        lax.fori_loop(0, EL, put, 0, unroll=4)
+    store_f = pltpu.make_async_copy(outv, out_f, lsem.at[7])
+    store_f.start()
+
     with jax.named_scope('prod_l'):
         beside(1)
-    with jax.named_scope('settle'):
-        for x_a, b in ((x_prev, 0), (x_next, 0), (x_prev, 1), (x_next, 1), (x, 0), (x, 1)):
-            settle(x_a, b)
+    with jax.named_scope('settle_l'):
+        settle(x_prev, 1)
+        settle(x_next, 1)
     far_unit(0)
+    with jax.named_scope('settle_f0'):
+        settle(x_far, 0)
     far_unit(1)
-    with jax.named_scope('settle_far'):
-        settle(x_far, 0)
+    with jax.named_scope('settle_f1'):
         settle(x_far, 1)
 
     with jax.named_scope('gather_y'):
@@ -394,24 +408,20 @@
         bytes_of(rz, rrecv).wait()
     for d in range(7):
         total = total + rz[d].astype(F32)
-    total = total * (1.0 / 65536.0)
-    mv[...] = total
-
-    def f_copy(s, to):
-        return remote(ft.at[s], fr.at[to], fsend.at[s], frecv.at[to], mirror_id(s))
+    mv[...] = total * (1.0 / 65536.0)
 
     @pl.when(mirrored)
     def _():
-        turned = total.T.astype(BF)
+        with jax.named_scope('w_mirror'):
+            bytes_of(fr, frecv).wait()
+        parts = []
         for s in range(4):
-            ft[s] = turned[s * 64 : s * 64 + 64]
-            f_copy(s, e % 4).start()
-        with jax.named_scope('w_mirror'):
-            for s in range(4):
-                f_copy(s, s).wait_recv()
-        mv[...] = mv[...] + jnp.concatenate([fr[s].astype(F32) for s in range(4)], axis=1)
-        for s in range(4):
-            f_copy(s, e % 4).wait_send()
+            part = fr[s, 0].astype(F32)
+            for other in range(1, 8):
+                part = part + fr[s, other].astype(F32)
+            parts.append(part)
+        mv[...] = mv[...] + jnp.concatenate(parts, axis=1) * (1.0 / 65536.0)
+        bytes_of(fr, fsend).wait()
 
     store_m = pltpu.make_async_copy(mv, out_m, lsem.at[8])
     store_m.start()
@@ -473,8 +483,8 @@
             pltpu.VMEM((2, 2, 2, 64, BD), BF),
             pltpu.VMEM((7, 64, BD), BF),
             pltpu.VMEM((64, BD), F32),
-            pltpu.VMEM((4, 64, 64), BF),
-            pltpu.VMEM((4, 64, 64), BF),
+            pltpu.VMEM((2, 2, 2, 4, 64, 64), BF),
+            pltpu.VMEM((4, 8, 64, 64), BF),
             dma((9,)),
             dma((2, 2, 2)), dma((2, 2, 2)),
             dma((2, 2)), dma((2, NCH)),
@@ -483,7 +493,7 @@
             dma, dma((4, 2)),
             dma, dma((3, 2)),
             dma, dma,
-            dma((4,)), dma((4,)),
+            dma, dma,
         ],
         compiler_params=pltpu.CompilerParams(collective_id=0, has_side_effects=True),
         name="chain",

time: 87.9 us -> 103 us (1.17)
  Pallas kernels: 84.1 us -> 99.7 us
    pallas_call x1, Pallas kernels: 84.1 us -> 99.7 us  [on_device(): pl.pallas_call(main_kernel, out_shape=(jax.ShapeDtypeStruct((EL, BMAX, BD...]
where the time goes in v7:
time: 103 us
  Pallas kernels  99.7 us (97%)
  local copies, waits for them, and re-layouts  2.97 us (3%)
    pallas_call x1, Pallas kernels, on_device(): pl.pallas_call(main_kernel, out_shape=(jax.ShapeDtypeStruct((EL, BMAX, BD...  99.7 us
    unnamed x4, local copies, waits for them, and re-layouts  2.97 us

profile of v7, /device:TPU:71, one launch (start us, length us, event | category | flops | bytes accessed | tf_op | source)
XLA Modules:
  0.0 103.3 jit_solution(1663296826485305139)
XLA Ops:
  0.6 99.7 %chain.1 = (bf16[32,64,256]{2,1,0:T(8,128)(2,1)}, f32[64,256]{1,0:T(8,128)}) custom-call(s32[4,32]{1,0:T(4,128)} %bitcast.1, s32[32]{0:T(128)} %size_h.1, bf16[32,64,256]{2,1,0:T(8,128)(2,1)} %yc_h.1, bf16[32,64,256]{2,1,0:T(8,128)(2,1)} %yp_h.1, bf16[32,64,320]{2,1,0:T(8,128)(2,1)} %h_h.1), custom_call_target="tpu_custom_call" | custom-call | tf_op jit(solution)/shard_map/chain/pallas_call | solution.py:451
  100.4 0.0 copy-start
  100.4 2.3 %copy.9 = bf16[32,64,256]{2,1,0:T(8,128)(2,1)} copy(bf16[32,64,256]{2,1,0:T(8,128)(2,1)} %get-tuple-element.4) | data formatting | bytes 2097152
  102.7 0.0 copy-done
  102.7 0.6 copy.10
Async XLA Ops:
  100.4 2.3 %copy-start = (f32[64,256]{1,0:T(8,128)S(1)}, f32[64,256]{1,0:T(8,128)}, u32[]{:S(2)}) copy-start(f32[64,256]{1,0:T(8,128)} %get-tuple-element.5) | copy-start | bytes 196612

commit v8 on v5

--- a/solution.py
+++ b/solution.py
@@ -180,21 +180,25 @@
 
         lax.fori_loop(row * GY, row * GY + GY, one, 0, unroll=8)
 
-    def z_copy(half, b, j):
-        return remote(
-            fil.at[b, pl.ds(half * GY + j * CH, CH)], xg.at[b, zh, pl.ds(j * CH, CH)],
-            zsend.at[half, b], zrecv.at[b, j], z_id((zl + 2 + 4 * half) % 8),
-        )
-
-    def x_copy(way, b, j):
+    def z_copy(b, j):
+        return remote(
+            fil.at[b, pl.ds((1 - zh) * GY + j * CH, CH)], xg.at[b, zh, pl.ds(j * CH, CH)],
+            zsend.at[b], zrecv.at[b, j], {"zh": 1 - zh},
+        )
+
+    def x_copy(way, b, j, kind):
         part = pl.ds(j * CH, CH)
-        return remote(
-            xg.at[b, :, part], (x1, x2)[way].at[b, :, part], xsend.at[way, b], xrecv.at[way, b, j], (xp, xm)[way]
-        )
-
-    def pass_on(b, j):
-        part, way = pl.ds(j * CH, CH), j // 2
-        return remote((x1, x2)[way].at[b, :, part], x3.at[b, :, part], gsend.at[b], grecv.at[b, j], (xp, xm)[way])
+        h = (zh, 1 - zh)[kind]
+        src = fil.at[b, pl.ds(zh * GY + j * CH, CH)] if kind == 0 else xg.at[b, h, part]
+        return remote(
+            src, (x1, x2)[way].at[b, h, part], xsend.at[way, b], xrecv.at[way, b, j, kind], (xp, xm)[way]
+        )
+
+    def pass_on(b, j, kind):
+        part, way, h = pl.ds(j * CH, CH), j // 2, (zh, 1 - zh)[kind]
+        return remote(
+            (x1, x2)[way].at[b, h, part], x3.at[b, h, part], gsend.at[b], grecv.at[b, j, kind], (xp, xm)[way]
+        )
 
     def bytes_of(ref, sem):
         return pltpu.make_async_copy(ref, ref, sem)
@@ -202,22 +206,26 @@
     def z_to_x(b):
         for j in ORDER:
             with jax.named_scope(f'wz{b}{j}'):
-                bytes_of(xg.at[b, :, pl.ds(j * CH, CH)], zrecv.at[b, j]).wait()
-            x_copy(0, b, j).start()
-            x_copy(1, b, j).start()
+                z_copy(b, j).wait_recv()
+            x_copy(0, b, j, 1).start()
+            x_copy(1, b, j, 1).start()
 
     def second(b):
-        def one(k, _):
-            j = (k % 2) * 2 + k // 2
+        for j in ORDER:
             for row in (1, 0):
                 for m in range(CH):
                     p = row * GY + j * CH + m
                     fil[b, p] = full_value(1, row, b, p)
-            for row in (1, 0):
-                z_copy(row, b, j).start()
-            return 0
-
-        lax.fori_loop(0, NCH, one, 0)
+            z_copy(b, j).start()
+            x_copy(0, b, j, 0).start()
+            x_copy(1, b, j, 0).start()
+        xg[b, zh] = fil[b, pl.ds(zh * GY, GY)]
+
+    def pass_half(b, kind):
+        for j in ORDER:
+            with jax.named_scope(f'wx{b}{kind}{j}'):
+                x_copy(j // 2, b, j, kind).wait_recv()
+            pass_on(b, j, kind).start()
 
     for b in (0, 1):
         with jax.named_scope(f'local0{b}'):
@@ -247,13 +255,16 @@
     @pl.when(outer)
     def _():
         z_to_x(0)
+        pass_half(0, 0)
 
     finish(1)
 
     @pl.when(jnp.logical_not(outer))
     def _():
         z_to_x(0)
-
+        pass_half(0, 0)
+
+    pass_half(1, 0)
     z_to_x(1)
 
     def put(i, _):
@@ -265,12 +276,6 @@
         lax.fori_loop(0, EL, put, 0, unroll=4)
     store_f = pltpu.make_async_copy(outv, out_f, lsem.at[7])
     store_f.start()
-
-    def pass_half(b):
-        for j in ORDER:
-            with jax.named_scope(f'wx{b}{j}'):
-                x_copy(j // 2, b, j).wait_recv()
-            pass_on(b, j).start()
 
     def bound_for(x_a, b):
         return (x_a % 2) * 2 + b
@@ -332,18 +337,20 @@
         for way in (0, 1):
             with jax.named_scope(f'w_x{way}'):
                 for j in ((2, 3), (0, 1))[way]:
-                    x_copy(way, b, j).wait_recv()
+                    for kind in (0, 1):
+                        x_copy(way, b, j, kind).wait_recv()
             product((x_prev, x_next)[way], b, (x1, x2)[way])
 
     def far_unit(b):
         with jax.named_scope(f'w_far{b}'):
             for j in ORDER:
-                pass_on(b, j).wait_recv()
+                for kind in (0, 1):
+                    pass_on(b, j, kind).wait_recv()
         product(x_far, b, x3)
         settle(x_far, b)
 
     same = y // 2 == x % 2
-    pass_half(0)
+    pass_half(0, 1)
     with jax.named_scope('prod_e'):
         product(x, 0, xg)
         product(x, 1, xg)
@@ -353,7 +360,7 @@
         settle(x, 1)
         settle(x_prev, 0)
         settle(x_next, 0)
-    pass_half(1)
+    pass_half(1, 1)
     with jax.named_scope('prod_l'):
         beside(1)
     with jax.named_scope('settle_l'):
@@ -393,9 +400,9 @@
                     halo_copy(degree, row, b).wait_send()
         for b in (0, 1):
             for k in (0, 1):
-                bytes_of(fil.at[b, pl.ds(k * GY, GY)], zsend.at[k, b]).wait()
                 bytes_of(xg.at[b], xsend.at[k, b]).wait()
             bytes_of(x3.at[b], gsend.at[b]).wait()
+            bytes_of(fil.at[b, pl.ds(0, GY)], zsend.at[b]).wait()
         bytes_of(rc, csend).wait()
         bytes_of(ry, ysend).wait()
         bytes_of(rz, rsend).wait()
@@ -445,9 +452,9 @@
             pltpu.VMEM((64, BD), F32),
             dma((9,)),
             dma((2, 2, 2)), dma((2, 2, 2)),
-            dma((2, 2)), dma((2, NCH)),
-            dma((2, 2)), dma((2, 2, NCH)),
             dma((2,)), dma((2, NCH)),
+            dma((2, 2)), dma((2, 2, NCH, 2)),
+            dma((2,)), dma((2, NCH, 2)),
             dma, dma((4, 2)),
             dma, dma((3, 2)),
             dma, dma,

time: 86.4 us -> 83.2 us (0.963)
  Pallas kernels: 82.4 us -> 79.2 us
    pallas_call x1, Pallas kernels: 82.4 us -> 79.2 us  [on_device(): pl.pallas_call(main_kernel, out_shape=(jax.ShapeDtypeStruct((EL, BMAX, BD...]
where the time goes in v8:
time: 83.2 us; the launch traced here: 82.8 us
  Pallas kernels  79.2 us (95%)
  local copies, waits for them, and re-layouts  2.97 us (4%)
    pallas_call x1, Pallas kernels, on_device(): pl.pallas_call(main_kernel, out_shape=(jax.ShapeDtypeStruct((EL, BMAX, BD...  79.2 us
    unnamed x4, local copies, waits for them, and re-layouts  2.97 us

profile of v8, /device:TPU:40, one launch (start us, length us, event | category | flops | bytes accessed | tf_op | source)
XLA Modules:
  0.0 82.8 jit_solution(14753685533397877221)
XLA Ops:
  0.6 79.2 %chain.1 = (bf16[32,64,256]{2,1,0:T(8,128)(2,1)}, f32[64,256]{1,0:T(8,128)}) custom-call(s32[4,32]{1,0:T(4,128)} %bitcast.1, s32[32]{0:T(128)} %size_h.1, bf16[32,64,256]{2,1,0:T(8,128)(2,1)} %yc_h.1, bf16[32,64,256]{2,1,0:T(8,128)(2,1)} %yp_h.1, bf16[32,64,320]{2,1,0:T(8,128)(2,1)} %h_h.1), custom_call_target="tpu_custom_call" | custom-call | tf_op jit(solution)/shard_map/chain/pallas_call | solution.py:418
  79.8 0.0 copy-start
  79.8 2.3 %copy.9 = bf16[32,64,256]{2,1,0:T(8,128)(2,1)} copy(bf16[32,64,256]{2,1,0:T(8,128)(2,1)} %get-tuple-element.4) | data formatting | bytes 2097152
  82.2 0.0 copy-done
  82.2 0.6 copy.10
Async XLA Ops:
  79.8 2.3 %copy-start = (f32[64,256]{1,0:T(8,128)S(1)}, f32[64,256]{1,0:T(8,128)}, u32[]{:S(2)}) copy-start(f32[64,256]{1,0:T(8,128)} %get-tuple-element.5) | copy-start | bytes 196612

commit v9 on v8

--- a/solution.py
+++ b/solution.py
@@ -66,13 +66,16 @@
     nb_h, size_h, yc_h, yp_h, h_h, out_f, out_m, nb, sizes, tbl, slot, link, power,
     yc, yp, hv, cur0, cur1, f000, f001, f010, f011, f100, f101, f110, f111,
     acc, fil, outv, xg, x1, x2, x3, pb, rc, s1, ry, s2, rz, mv,
-    lsem, hsend, hrecv, zsend, zrecv, xsend, xrecv, gsend, grecv, csend, crecv, ysend, yrecv, rsend, rrecv,
+    lsem, hsend, hrecv, zsend, zrecv, xsend, xrecv, gsend, grecv, csend, crecv, ysend, yrecv, rsend, rrecv, gate,
 ):
     zl, y, c = (lax.axis_index(a) for a in ELEM)
     zh, x = (lax.axis_index(a) for a in BAND)
     z = zh * 4 + zl
     e = (zl * 4 + y) * 2 + c
     outer = jnp.logical_or(y == 0, y == 3)
+    crossing = jnp.logical_or(jnp.logical_and(y == 0, c == 0), jnp.logical_and(y == 3, c == 1))
+    last = jnp.logical_or(jnp.logical_and(y == 0, zl == 0), jnp.logical_and(y == 3, zl == 3))
+    held = jnp.logical_and(outer, jnp.logical_not(last))
 
     def elem_id(other):
         return {"zl": other // 8, "y": (other // 2) % 4, "c": other % 2}
@@ -216,7 +219,14 @@
                 for m in range(CH):
                     p = row * GY + j * CH + m
                     fil[b, p] = full_value(1, row, b, p)
-            z_copy(b, j).start()
+            if b == 0:
+
+                @pl.when(jnp.logical_not(held))
+                def _():
+                    z_copy(b, j).start()
+
+            else:
+                z_copy(b, j).start()
             x_copy(0, b, j, 0).start()
             x_copy(1, b, j, 0).start()
         xg[b, zh] = fil[b, pl.ds(zh * GY, GY)]
@@ -247,23 +257,30 @@
         with jax.named_scope(f'w_h1{b}'):
             halo_copy(1, 1, b).wait_recv()
             halo_copy(1, 0, b).wait_recv()
+        if b == 1:
+
+            @pl.when(jnp.logical_and(crossing, held))
+            def _():
+                pl.semaphore_signal(gate, inc=1, device_id={"c": 1 - c}, device_id_type=MESH_ID)
+
+            @pl.when(jnp.logical_and(held, jnp.logical_not(crossing)))
+            def _():
+                with jax.named_scope('w_gate'):
+                    pl.semaphore_wait(gate, 1)
+
+            @pl.when(held)
+            def _():
+                for j in ORDER:
+                    z_copy(0, j).start()
+
         with jax.named_scope(f'second{b}'):
             second(b)
 
     finish(0)
 
-    @pl.when(outer)
-    def _():
-        z_to_x(0)
-        pass_half(0, 0)
-
     finish(1)
-
-    @pl.when(jnp.logical_not(outer))
-    def _():
-        z_to_x(0)
-        pass_half(0, 0)
-
+    z_to_x(0)
+    pass_half(0, 0)
     pass_half(1, 0)
     z_to_x(1)
 
@@ -458,6 +475,7 @@
             dma, dma((4, 2)),
             dma, dma((3, 2)),
             dma, dma,
+            pltpu.SemaphoreType.REGULAR,
         ],
         compiler_params=pltpu.CompilerParams(collective_id=0, has_side_effects=True),
         name="chain",

time: 83.2 us -> 80.6 us (0.969)
  Pallas kernels: 79.2 us -> 76.8 us
    pallas_call x1, Pallas kernels: 79.2 us -> 76.8 us  [on_device(): pl.pallas_call(main_kernel, out_shape=(jax.ShapeDtypeStruct((EL, BMAX, BD...]
where the time goes in v9:
time: 80.6 us; the launch traced here: 80.5 us
  Pallas kernels  76.8 us (95%)
  local copies, waits for them, and re-layouts  2.97 us (4%)
    pallas_call x1, Pallas kernels, on_device(): pl.pallas_call(main_kernel, out_shape=(jax.ShapeDtypeStruct((EL, BMAX, BD...  76.8 us
    unnamed x4, local copies, waits for them, and re-layouts  2.97 us

profile of v9, /device:TPU:40, one launch (start us, length us, event | category | flops | bytes accessed | tf_op | source)
XLA Modules:
  0.0 80.5 jit_solution(242810709300414621)
XLA Ops:
  0.6 76.8 %chain.1 = (bf16[32,64,256]{2,1,0:T(8,128)(2,1)}, f32[64,256]{1,0:T(8,128)}) custom-call(s32[4,32]{1,0:T(4,128)} %bitcast.1, s32[32]{0:T(128)} %size_h.1, bf16[32,64,256]{2,1,0:T(8,128)(2,1)} %yc_h.1, bf16[32,64,256]{2,1,0:T(8,128)(2,1)} %yp_h.1, bf16[32,64,320]{2,1,0:T(8,128)(2,1)} %h_h.1), custom_call_target="tpu_custom_call" | custom-call | tf_op jit(solution)/shard_map/chain/pallas_call | solution.py:435
  77.5 0.0 copy-start
  77.5 2.3 %copy.9 = bf16[32,64,256]{2,1,0:T(8,128)(2,1)} copy(bf16[32,64,256]{2,1,0:T(8,128)(2,1)} %get-tuple-element.4) | data formatting | bytes 2097152
  79.8 0.0 copy-done
  79.8 0.6 copy.10
Async XLA Ops:
  77.5 2.3 %copy-start = (f32[64,256]{1,0:T(8,128)S(1)}, f32[64,256]{1,0:T(8,128)}, u32[]{:S(2)}) copy-start(f32[64,256]{1,0:T(8,128)} %get-tuple-element.5) | copy-start | bytes 196612

commit v10 on v9

--- a/solution.py
+++ b/solution.py
@@ -66,7 +66,7 @@
     nb_h, size_h, yc_h, yp_h, h_h, out_f, out_m, nb, sizes, tbl, slot, link, power,
     yc, yp, hv, cur0, cur1, f000, f001, f010, f011, f100, f101, f110, f111,
     acc, fil, outv, xg, x1, x2, x3, pb, rc, s1, ry, s2, rz, mv,
-    lsem, hsend, hrecv, zsend, zrecv, xsend, xrecv, gsend, grecv, csend, crecv, ysend, yrecv, rsend, rrecv, gate,
+    lsem, hsend, hrecv, zsend, zrecv, xsend, xrecv, gsend, grecv, csend, crecv, ysend, yrecv, rsend, rrecv,
 ):
     zl, y, c = (lax.axis_index(a) for a in ELEM)
     zh, x = (lax.axis_index(a) for a in BAND)
@@ -259,15 +259,6 @@
             halo_copy(1, 0, b).wait_recv()
         if b == 1:
 
-            @pl.when(jnp.logical_and(crossing, held))
-            def _():
-                pl.semaphore_signal(gate, inc=1, device_id={"c": 1 - c}, device_id_type=MESH_ID)
-
-            @pl.when(jnp.logical_and(held, jnp.logical_not(crossing)))
-            def _():
-                with jax.named_scope('w_gate'):
-                    pl.semaphore_wait(gate, 1)
-
             @pl.when(held)
             def _():
                 for j in ORDER:
@@ -297,36 +288,34 @@
     def bound_for(x_a, b):
         return (x_a % 2) * 2 + b
 
-    def c_copy(x_a, b):
-        at = (pl.ds(0, 2), x_a // 2, bound_for(x_a, b))
-        return remote(pb.at[(1 - c, *at)], rc.at[at], csend, crecv.at[x_a, b], {"c": 1 - c})
-
-    def product(x_a, b, ref):
-        left = jnp.concatenate([ref[b, h].reshape(GY * BMAX, HB) for h in (0, 1)], axis=1)
+    def c_copy(x_a, b, kind):
+        at = ((zh, 1 - zh)[kind], x_a // 2, bound_for(x_a, b))
+        return remote(pb.at[(1 - c, *at)], rc.at[at], csend, crecv.at[x_a, b, kind], {"c": 1 - c})
+
+    def product(x_a, b, kind, ref):
+        zh_a = (zh, 1 - zh)[kind]
+        left = ref[b, zh_a].reshape(GY * BMAX, HB)
         for zh_b in (0, 1):
             right = jnp.concatenate([xg[k, zh_b].reshape(GY * BMAX, HB) for k in (0, 1)], axis=1)
             tile = lax.dot_general(left, right, (((0,), (0,)), ((), ())), preferred_element_type=F32).astype(BF)
-            for zh_a in (0, 1):
-                for core in (0, 1):
-                    at = zh_a * HB + core * 64
-                    pb[core, zh_a, x_a // 2, bound_for(x_a, b), zh_b] = tile[at : at + 64]
-        c_copy(x_a, b).start()
-
-    def y_copy(to, d, xh):
+            for core in (0, 1):
+                pb[core, zh_a, x_a // 2, bound_for(x_a, b), zh_b] = tile[core * 64 : core * 64 + 64]
+        c_copy(x_a, b, kind).start()
+
+    def y_copy(to, d, xh, kind):
+        zh_a = (zh, 1 - zh)[kind]
         return remote(
-            s1.at[:, xh, to], ry.at[d - 1, xh], ysend, yrecv.at[d - 1, xh], {"y": to}
-        )
-
-    def settle(x_a, b):
-        xh, to = x_a // 2, bound_for(x_a, b)
-        with jax.named_scope(f'wc{b}'):
-            c_copy(x_a, b).wait_recv()
-        for zh_a in (0, 1):
-            s1[zh_a, xh, to] = (pb[c, zh_a, xh, to].astype(F32) + rc[zh_a, xh, to].astype(F32)).astype(BF)
+            s1.at[zh_a, xh, to], ry.at[d - 1, xh, zh_a], ysend, yrecv.at[d - 1, xh, kind], {"y": to}
+        )
+
+    def settle(x_a, b, kind):
+        zh_a, xh, to = (zh, 1 - zh)[kind], x_a // 2, bound_for(x_a, b)
+        c_copy(x_a, b, kind).wait_recv()
+        s1[zh_a, xh, to] = (pb[c, zh_a, xh, to].astype(F32) + rc[zh_a, xh, to].astype(F32)).astype(BF)
 
         @pl.when(to != y)
         def _():
-            y_copy(to, (to + 4 - y) % 4, xh).start()
+            y_copy(to, (to + 4 - y) % 4, xh, kind).start()
 
     def r_copy(to, src_xh):
         d = (to + 8 - z) % 8
@@ -336,7 +325,8 @@
 
     def gather_y(xh):
         for d in (1, 3, 2):
-            y_copy((y + d) % 4, d, xh).wait_recv()
+            for kind in (0, 1):
+                y_copy((y + d) % 4, d, xh, kind).wait_recv()
         for zh_a in (0, 1):
             total = s1[zh_a, xh, y].astype(F32)
             for d in range(3):
@@ -350,41 +340,58 @@
                 def _():
                     r_copy(to, xh).start()
 
-    def beside(b):
+    def wait_beside(b, kind):
         for way in (0, 1):
-            with jax.named_scope(f'w_x{way}'):
-                for j in ((2, 3), (0, 1))[way]:
-                    for kind in (0, 1):
-                        x_copy(way, b, j, kind).wait_recv()
-            product((x_prev, x_next)[way], b, (x1, x2)[way])
-
-    def far_unit(b):
-        with jax.named_scope(f'w_far{b}'):
-            for j in ORDER:
-                for kind in (0, 1):
-                    pass_on(b, j, kind).wait_recv()
-        product(x_far, b, x3)
-        settle(x_far, b)
+            for j in ((2, 3), (0, 1))[way]:
+                x_copy(way, b, j, kind).wait_recv()
+
+    def wait_far(b, kind):
+        for j in ORDER:
+            pass_on(b, j, kind).wait_recv()
+
+    def all_of(units):
+        for unit, ref in units:
+            product(*unit, ref)
+        return [unit for unit, _ in units]
+
+    def settle_all(units):
+        for unit in units:
+            settle(*unit)
+
+    def beside(b, kind):
+        return [((x_prev, b, kind), x1), ((x_next, b, kind), x2)]
 
     same = y // 2 == x % 2
     pass_half(0, 1)
     with jax.named_scope('prod_e'):
-        product(x, 0, xg)
-        product(x, 1, xg)
-        beside(0)
+        for b in (0, 1):
+            wait_beside(b, 0)
+        early = all_of([((x, b, kind), xg) for b in (0, 1) for kind in (0, 1)] + beside(0, 0) + beside(1, 0))
     with jax.named_scope('settle_e'):
-        settle(x, 0)
-        settle(x, 1)
-        settle(x_prev, 0)
-        settle(x_next, 0)
+        settle_all(early)
+    with jax.named_scope('w_x0'):
+        wait_beside(0, 1)
+    with jax.named_scope('prod_m'):
+        middle = all_of(beside(0, 1))
     pass_half(1, 1)
+    with jax.named_scope('w_far_0'):
+        wait_far(0, 0)
+        wait_far(1, 0)
+    with jax.named_scope('prod_f0'):
+        middle += all_of([((x_far, 0, 0), x3), ((x_far, 1, 0), x3)])
+    with jax.named_scope('settle_m'):
+        settle_all(middle)
+    with jax.named_scope('w_x1'):
+        wait_beside(1, 1)
     with jax.named_scope('prod_l'):
-        beside(1)
-    with jax.named_scope('settle_l'):
-        settle(x_prev, 1)
-        settle(x_next, 1)
-    far_unit(0)
-    far_unit(1)
+        late = all_of(beside(1, 1))
+        settle_all(late)
+    with jax.named_scope('w_far0'):
+        wait_far(0, 1)
+    settle_all(all_of([((x_far, 0, 1), x3)]))
+    with jax.named_scope('w_far1'):
+        wait_far(1, 1)
+    settle_all(all_of([((x_far, 1, 1), x3)]))
 
     with jax.named_scope('gather_y1'):
         @pl.when(same)
@@ -427,12 +434,31 @@
         store_m.wait()
 
 
+PARTS = 4
+
+
+def put_out_kernel(f_h, m_h, f_out, m_out, f_v, m_v, came, gone):
+    pairs = [(m_h, m_v, m_out)]
+    for k in range(PARTS):
+        part = pl.ds(k * EL // PARTS, EL // PARTS)
+        pairs.append((f_h.at[part], f_v.at[part], f_out.at[part]))
+    into = [pltpu.make_async_copy(a, b, came.at[k]) for k, (a, b, _) in enumerate(pairs)]
+    out = [pltpu.make_async_copy(b, a, gone.at[k]) for k, (_, b, a) in enumerate(pairs)]
+    for copy in into:
+        copy.start()
+    for first, then in zip(into, out):
+        first.wait()
+        then.start()
+    for copy in out:
+        copy.wait()
+
+
 def on_device(y_current, y_previous, h_blocks, basis_sizes, neighbours):
     any_space = pl.BlockSpec(memory_space=pl.ANY)
     dma = pltpu.SemaphoreType.DMA
     halves = pltpu.VMEM((2, EL, BMAX, HB), BF)
     met = pltpu.VMEM((2, 2, GY, BMAX, HB), BF)
-    return pl.pallas_call(
+    filtered, margin = pl.pallas_call(
         main_kernel,
         out_shape=(
             jax.ShapeDtypeStruct((EL, BMAX, BD), BF),
@@ -472,14 +498,28 @@
             dma((2,)), dma((2, NCH)),
             dma((2, 2)), dma((2, 2, NCH, 2)),
             dma((2,)), dma((2, NCH, 2)),
-            dma, dma((4, 2)),
-            dma, dma((3, 2)),
+            dma, dma((4, 2, 2)),
+            dma, dma((3, 2, 2)),
             dma, dma,
-            pltpu.SemaphoreType.REGULAR,
         ],
         compiler_params=pltpu.CompilerParams(collective_id=0, has_side_effects=True),
         name="chain",
     )(neighbours.T, basis_sizes, y_current, y_previous, h_blocks)
+    return pl.pallas_call(
+        put_out_kernel,
+        out_shape=(
+            jax.ShapeDtypeStruct((EL, BMAX, BD), BF),
+            jax.ShapeDtypeStruct((64, BD), F32),
+        ),
+        in_specs=[any_space] * 2,
+        out_specs=(any_space, any_space),
+        scratch_shapes=[
+            pltpu.VMEM((EL, BMAX, BD), BF),
+            pltpu.VMEM((64, BD), F32),
+            dma((PARTS + 1,)), dma((PARTS + 1,)),
+        ],
+        name="put_out",
+    )(filtered, margin)
 
 
 def solution(mesh):

time: 80.6 us -> 78 us (0.968)
  local copies, waits for them, and re-layouts: 2.97 us -> 0 us
    unnamed x4 -> x0, local copies, waits for them, and re-layouts: 2.97 us -> none
    pallas_call x0 -> x1, Pallas kernels: none -> 2.04 us  [on_device(): pl.pallas_call(put_out_kernel, out_shape=(jax.ShapeDtypeStruct((EL, BMAX,...]
    pallas_call x1, Pallas kernels: 76.8 us -> 75.2 us  [on_device(): pl.pallas_call(main_kernel, out_shape=(jax.ShapeDtypeStruct((EL, BMAX, BD...]
where the time goes in v10:
time: 78 us; the launch traced here: 77.8 us
  Pallas kernels  77.2 us (99%)
    pallas_call x1, Pallas kernels, on_device(): pl.pallas_call(main_kernel, out_shape=(jax.ShapeDtypeStruct((EL, BMAX, BD...  75.2 us
    pallas_call x1, Pallas kernels, on_device(): pl.pallas_call(put_out_kernel, out_shape=(jax.ShapeDtypeStruct((EL, BMAX,...  2.04 us

profile of v10, /device:TPU:40, one launch (start us, length us, event | category | flops | bytes accessed | tf_op | source)
XLA Modules:
  0.0 77.8 jit_solution(2688143324974051685)
XLA Ops:
  0.6 75.2 %chain.1 = (bf16[32,64,256]{2,1,0:T(8,128)(2,1)}, f32[64,256]{1,0:T(8,128)}) custom-call(s32[4,32]{1,0:T(4,128)} %bitcast.1, s32[32]{0:T(128)} %size_h.1, bf16[32,64,256]{2,1,0:T(8,128)(2,1)} %yc_h.1, bf16[32,64,256]{2,1,0:T(8,128)(2,1)} %yp_h.1, bf16[32,64,320]{2,1,0:T(8,128)(2,1)} %h_h.1), custom_call_target="tpu_custom_call" | custom-call | tf_op jit(solution)/shard_map/chain/pallas_call | solution.py:461
  75.8 2.0 %put_out.1 = (bf16[32,64,256]{2,1,0:T(8,128)(2,1)}, f32[64,256]{1,0:T(8,128)}) custom-call(bf16[32,64,256]{2,1,0:T(8,128)(2,1)} %get-tuple-element.4.f_h, f32[64,256]{1,0:T(8,128)} %get-tuple-element.5.m_h), custom_call_target="tpu_custom_call" | custom-call | tf_op jit(solution)/shard_map/put_out/pallas_call | solution.py:508

commit v11 on v10

--- a/solution.py
+++ b/solution.py
@@ -75,7 +75,7 @@
     outer = jnp.logical_or(y == 0, y == 3)
     crossing = jnp.logical_or(jnp.logical_and(y == 0, c == 0), jnp.logical_and(y == 3, c == 1))
     last = jnp.logical_or(jnp.logical_and(y == 0, zl == 0), jnp.logical_and(y == 3, zl == 3))
-    held = jnp.logical_and(outer, jnp.logical_not(last))
+    at_once = jnp.where(last, 4, jnp.where(outer, 1, NCH))
 
     def elem_id(other):
         return {"zl": other // 8, "y": (other // 2) % 4, "c": other % 2}
@@ -221,12 +221,16 @@
                     fil[b, p] = full_value(1, row, b, p)
             if b == 0:
 
-                @pl.when(jnp.logical_not(held))
+                @pl.when(ORDER.index(j) < at_once)
                 def _():
                     z_copy(b, j).start()
 
             else:
-                z_copy(b, j).start()
+
+                @pl.when(jnp.logical_not(last))
+                def _():
+                    z_copy(b, j).start()
+
             x_copy(0, b, j, 0).start()
             x_copy(1, b, j, 0).start()
         xg[b, zh] = fil[b, pl.ds(zh * GY, GY)]
@@ -259,9 +263,10 @@
             halo_copy(1, 0, b).wait_recv()
         if b == 1:
 
-            @pl.when(held)
-            def _():
-                for j in ORDER:
+            for k, j in enumerate(ORDER):
+
+                @pl.when(k >= at_once)
+                def _():
                     z_copy(0, j).start()
 
         with jax.named_scope(f'second{b}'):
@@ -273,6 +278,12 @@
     z_to_x(0)
     pass_half(0, 0)
     pass_half(1, 0)
+
+    @pl.when(last)
+    def _():
+        for j in ORDER:
+            z_copy(1, j).start()
+
     z_to_x(1)
 
     def put(i, _):
@@ -323,22 +334,20 @@
             s2.at[src_xh, (to % 4) // 2, to // 4], rz.at[d - 1], rsend, rrecv, z_id(to)
         )
 
-    def gather_y(xh):
+    def gather_y(xh, kind):
+        zh_a = (zh, 1 - zh)[kind]
         for d in (1, 3, 2):
-            for kind in (0, 1):
-                y_copy((y + d) % 4, d, xh, kind).wait_recv()
-        for zh_a in (0, 1):
-            total = s1[zh_a, xh, y].astype(F32)
-            for d in range(3):
-                total = total + ry[d, xh, zh_a].astype(F32)
-            s2[xh, zh_a] = total.astype(BF)
-        for zh_a in (0, 1):
-            for zh_b in (0, 1):
-                to = zh_b * 4 + zh_a * 2 + xh
-
-                @pl.when(to != z)
-                def _():
-                    r_copy(to, xh).start()
+            y_copy((y + d) % 4, d, xh, kind).wait_recv()
+        total = s1[zh_a, xh, y].astype(F32)
+        for d in range(3):
+            total = total + ry[d, xh, zh_a].astype(F32)
+        s2[xh, zh_a] = total.astype(BF)
+        for zh_b in (0, 1):
+            to = zh_b * 4 + zh_a * 2 + xh
+
+            @pl.when(to != z)
+            def _():
+                r_copy(to, xh).start()
 
     def wait_beside(b, kind):
         for way in (0, 1):
@@ -361,7 +370,6 @@
     def beside(b, kind):
         return [((x_prev, b, kind), x1), ((x_next, b, kind), x2)]
 
-    same = y // 2 == x % 2
     pass_half(0, 1)
     with jax.named_scope('prod_e'):
         for b in (0, 1):
@@ -393,20 +401,13 @@
         wait_far(1, 1)
     settle_all(all_of([((x_far, 1, 1), x3)]))
 
+    with jax.named_scope('gather_y0'):
+        gather_y(x // 2, 0)
+        gather_y(1 - x // 2, 0)
     with jax.named_scope('gather_y1'):
-        @pl.when(same)
-        def _():
-            gather_y(x // 2)
-
-        @pl.when(jnp.logical_not(same))
-        def _():
-            gather_y(0)
-            gather_y(1)
-
+        gather_y(x // 2, 1)
     with jax.named_scope('gather_y2'):
-        @pl.when(same)
-        def _():
-            gather_y(1 - x // 2)
+        gather_y(1 - x // 2, 1)
 
     total = s2[zl % 2, zl // 2, zh].astype(F32)
     with jax.named_scope('wr'):

time: 78 us -> 75.4 us (0.967)
  the two profiles are of different devices: /device:TPU:40 before, /device:TPU:8 now
where the time goes in v11:
time: 75.4 us; the launch traced here: 75.2 us
  Pallas kernels  74.6 us (99%)
    pallas_call x1, Pallas kernels, on_device(): pl.pallas_call(main_kernel, out_shape=(jax.ShapeDtypeStruct((EL, BMAX, BD...  72.6 us
    pallas_call x1, Pallas kernels, on_device(): pl.pallas_call(put_out_kernel, out_shape=(jax.ShapeDtypeStruct((EL, BMAX,...  2.04 us

profile of v11, /device:TPU:8, one launch (start us, length us, event | category | flops | bytes accessed | tf_op | source)
XLA Modules:
  0.0 75.2 jit_solution(17527894005484577321)
XLA Ops:
  0.6 72.6 %chain.1 = (bf16[32,64,256]{2,1,0:T(8,128)(2,1)}, f32[64,256]{1,0:T(8,128)}) custom-call(s32[4,32]{1,0:T(4,128)} %bitcast.1, s32[32]{0:T(128)} %size_h.1, bf16[32,64,256]{2,1,0:T(8,128)(2,1)} %yc_h.1, bf16[32,64,256]{2,1,0:T(8,128)(2,1)} %yp_h.1, bf16[32,64,320]{2,1,0:T(8,128)(2,1)} %h_h.1), custom_call_target="tpu_custom_call" | custom-call | tf_op jit(solution)/shard_map/chain/pallas_call | solution.py:462
  73.2 2.0 %put_out.1 = (bf16[32,64,256]{2,1,0:T(8,128)(2,1)}, f32[64,256]{1,0:T(8,128)}) custom-call(bf16[32,64,256]{2,1,0:T(8,128)(2,1)} %get-tuple-element.4.f_h, f32[64,256]{1,0:T(8,128)} %get-tuple-element.5.m_h), custom_call_target="tpu_custom_call" | custom-call | tf_op jit(solution)/shard_map/put_out/pallas_call | solution.py:509

commit v12 on v11

--- a/solution.py
+++ b/solution.py
@@ -139,16 +139,20 @@
         )
 
     with jax.named_scope('pack'):
-        pack(1, 0)
+        for b in (0, 1):
+            pack(1, b)
+            pack(0, b)
     with jax.named_scope('barrier'):
         pl.semaphore_wait(barrier, len(partners))
-    halo_copy(0, 0, 0).start()
-    pack(0, 0)
-    halo_copy(0, 1, 0).start()
-    pack(1, 1)
-    halo_copy(0, 0, 1).start()
-    pack(0, 1)
-    halo_copy(0, 1, 1).start()
+
+    for core in (0, 1):
+
+        @pl.when(c == core)
+        def _():
+            for row in (1 - core, core):
+                for b in (0, 1):
+                    halo_copy(0, row, b).start()
+
     for load in loads[4:]:
         load.wait()
 

time: 75.4 us -> 75.2 us (level)
  the two profiles are of different devices: /device:TPU:8 before, /device:TPU:40 now
where the time goes in v12:
time: 75.2 us; the launch traced here: 73.9 us
  Pallas kernels  73.2 us (97%)
    pallas_call x1, Pallas kernels, on_device(): pl.pallas_call(main_kernel, out_shape=(jax.ShapeDtypeStruct((EL, BMAX, BD...  71.2 us
    pallas_call x1, Pallas kernels, on_device(): pl.pallas_call(put_out_kernel, out_shape=(jax.ShapeDtypeStruct((EL, BMAX,...  2.04 us

profile of v12, /device:TPU:40, one launch (start us, length us, event | category | flops | bytes accessed | tf_op | source)
XLA Modules:
  0.0 73.9 jit_solution(12846141162917645145)
XLA Ops:
  0.6 71.2 %chain.1 = (bf16[32,64,256]{2,1,0:T(8,128)(2,1)}, f32[64,256]{1,0:T(8,128)}) custom-call(s32[4,32]{1,0:T(4,128)} %bitcast.1, s32[32]{0:T(128)} %size_h.1, bf16[32,64,256]{2,1,0:T(8,128)(2,1)} %yc_h.1, bf16[32,64,256]{2,1,0:T(8,128)(2,1)} %yp_h.1, bf16[32,64,320]{2,1,0:T(8,128)(2,1)} %h_h.1), custom_call_target="tpu_custom_call" | custom-call | tf_op jit(solution)/shard_map/chain/pallas_call | solution.py:466
  71.8 2.0 %put_out.1 = (bf16[32,64,256]{2,1,0:T(8,128)(2,1)}, f32[64,256]{1,0:T(8,128)}) custom-call(bf16[32,64,256]{2,1,0:T(8,128)(2,1)} %get-tuple-element.4.f_h, f32[64,256]{1,0:T(8,128)} %get-tuple-element.5.m_h), custom_call_target="tpu_custom_call" | custom-call | tf_op jit(solution)/shard_map/put_out/pallas_call | solution.py:513

commit v13 on v12

--- a/solution.py
+++ b/solution.py
@@ -346,7 +346,7 @@
         for d in range(3):
             total = total + ry[d, xh, zh_a].astype(F32)
         s2[xh, zh_a] = total.astype(BF)
-        for zh_b in (0, 1):
+        for zh_b in (1 - zh, zh):
             to = zh_b * 4 + zh_a * 2 + xh
 
             @pl.when(to != z)

time: 75.2 us -> 75.2 us (level)
  no operation moved by 1% of the time
where the time goes in v13:
time: 75.2 us; the launch traced here: 73.9 us
  Pallas kernels  73.2 us (97%)
    pallas_call x1, Pallas kernels, on_device(): pl.pallas_call(main_kernel, out_shape=(jax.ShapeDtypeStruct((EL, BMAX, BD...  71.2 us
    pallas_call x1, Pallas kernels, on_device(): pl.pallas_call(put_out_kernel, out_shape=(jax.ShapeDtypeStruct((EL, BMAX,...  2.04 us

profile of v13, /device:TPU:40, one launch (start us, length us, event | category | flops | bytes accessed | tf_op | source)
XLA Modules:
  0.0 73.9 jit_solution(4836152176602751697)
XLA Ops:
  0.6 71.2 %chain.1 = (bf16[32,64,256]{2,1,0:T(8,128)(2,1)}, f32[64,256]{1,0:T(8,128)}) custom-call(s32[4,32]{1,0:T(4,128)} %bitcast.1, s32[32]{0:T(128)} %size_h.1, bf16[32,64,256]{2,1,0:T(8,128)(2,1)} %yc_h.1, bf16[32,64,256]{2,1,0:T(8,128)(2,1)} %yp_h.1, bf16[32,64,320]{2,1,0:T(8,128)(2,1)} %h_h.1), custom_call_target="tpu_custom_call" | custom-call | tf_op jit(solution)/shard_map/chain/pallas_call | solution.py:466
  71.8 2.0 %put_out.1 = (bf16[32,64,256]{2,1,0:T(8,128)(2,1)}, f32[64,256]{1,0:T(8,128)}) custom-call(bf16[32,64,256]{2,1,0:T(8,128)(2,1)} %get-tuple-element.4.f_h, f32[64,256]{1,0:T(8,128)} %get-tuple-element.5.m_h), custom_call_target="tpu_custom_call" | custom-call | tf_op jit(solution)/shard_map/put_out/pallas_call | solution.py:513
